TPU v7x, 32 devices: a whole 2x2x4 slice. The times are simulated.
32 devices in a mesh: grp: 8 (over z, y), dev: 4 (over x, core).
Axes of the slice: x: 2, y: 2, z: 4, core: 2. Of those that a mesh axis runs over, the one named last changes fastest.
Arguments:
- right_side: float32 [8, 4, 3, 4096], P('grp', 'dev'), may hold values from -15 to 15
- elem_nodes: int32 [8, 4, 27, 512], P('grp', 'dev'), may hold values from 0 to 4095, as said below
- elem_coef: float32 [8, 4, 512], P('grp', 'dev'), may hold values from 0.2 to 5
- node_mass: float32 [8, 4, 3, 4096], P('grp', 'dev'), may hold values from 0.5 to 4
- face_slots: int32 [8, 4, 4, 512], P('grp', 'dev'), may hold values from 0 to 4096, as said below
- coarse_nodes: int32 [8, 4, 4, 4096], P('grp', 'dev'), may hold values from 0 to 1535, as said below
- coarse_weights: float32 [8, 4, 4, 4096], P('grp', 'dev'), may hold values from 0.1 to 0.6
- elem_matrix: float32 [81, 81], replicated, may hold values from -1 to 2, as said below
- chol_inverse: float32 [4608, 4608], P('dev'), may hold values from -1 to 1, as said below
Outputs:
- preconditioned: float32 [8, 4, 3, 4096], P('grp', 'dev')
Inputs may be any that keep to these rules, and one draw needn't show every extreme that they name: `elem_nodes`: the 27 entries of one element are distinct. `face_slots`: an entry 4096 is padding; the other entries of one subdomain are distinct. Slot p of a face and slot p of the neighbour's face back name the same shared node: both are padding or neither. Live slots come first in a face; faces with no neighbour subdomain are all padding; some face has all 512 slots live. `coarse_nodes`: the entries of subdomain (g, d) lie in the 64 coarse nodes from ((4 * g + d) * 1536) // 32 on, counted modulo 1536. `elem_matrix`: Symmetric; each diagonal entry is positive and exceeds the sum of the magnitudes of the other entries of its row. `chol_inverse`: lower triangular with a positive diagonal.
All inputs are finite; a program needn't handle non-finite values.
Results may differ from a plain program's by a relative error of at most 0.0001.
Values sent between devices are 32-bit elements; how exact they have to be, the bound alone decides.
No kernel may reach another device: no remote copies, remote signals or barrier semaphores. Data moves between devices by JAX's collectives and lax.ppermute only.
A program may use at most 128 MiB of HBM per device.

v0:
```python
import jax
import jax.numpy as jnp
from jax import lax
from jax.sharding import PartitionSpec as P

POST = 2


DAMPING = 0.6
PRECISE = lax.Precision.HIGHEST


def from_behind(value, axis, steps):
    count = lax.axis_size(axis)
    initial, last = (max(0, -steps), min(count, count - steps))
    return lax.ppermute(value, axis, [(source, source + steps) for source in range(initial, last)])


def element_apply(matrix, field, node_index, elem_scale, mass_here):
    elem_count = node_index.shape[1]
    gathered = field[:, node_index].reshape(81, elem_count)
    product = jnp.dot(matrix, gathered, precision=PRECISE) * elem_scale[None, :]
    summed = jnp.zeros_like(field).at[:, node_index].add(product.reshape(3, 27, elem_count))
    return summed + mass_here * field


def exchange_faces(field, face_index):
    outgoing = field.at[:, face_index].get(mode="fill", fill_value=0.0)
    from_below = from_behind(outgoing[:, 1], "grp", 1)
    from_above = from_behind(outgoing[:, 0], "grp", -1)
    from_left = from_behind(outgoing[:, 3], "dev", 1)
    from_right = from_behind(outgoing[:, 2], "dev", -1)
    received = jnp.stack([from_below, from_above, from_left, from_right], axis=1)
    return field.at[:, face_index].add(received, mode="drop")


def restrict(coarse_width, field, coarse_index, weights):
    values = weights[None] * field[:, None, :]
    return (
        jnp.zeros((3, coarse_width), field.dtype)
        .at[:, coarse_index]
        .add(values)
        .reshape(3 * coarse_width)
    )


def prolong(coarse, coarse_index, weights):
    coarse_table = coarse.reshape(3, coarse.shape[0] // 3)
    return jnp.sum(weights[None] * coarse_table[:, coarse_index], axis=1)


def local(
    right_side,
    elem_nodes,
    elem_coef,
    node_mass,
    face_slots,
    coarse_nodes,
    coarse_weights,
    elem_matrix,
    chol_inverse,
):
    target = right_side[0, 0]
    node_index = elem_nodes[0, 0]
    elem_scale = elem_coef[0, 0]
    mass_here = node_mass[0, 0]
    face_index = face_slots[0, 0]
    coarse_index = coarse_nodes[0, 0]
    weights = coarse_weights[0, 0]
    coarse_width = chol_inverse.shape[1] // 3

    def operate(field):
        return exchange_faces(
            element_apply(elem_matrix, field, node_index, elem_scale, mass_here), face_index
        )

    main_diag = jnp.diagonal(elem_matrix).reshape(3, 27)
    local_diag = (
        jnp.zeros_like(mass_here)
        .at[:, node_index]
        .add(main_diag[:, :, None] * elem_scale[None, None, :])
        + mass_here
    )
    diag_total = exchange_faces(local_diag, face_index)
    iterate = DAMPING * target / diag_total
    iterate = iterate + DAMPING * (target - operate(iterate)) / diag_total
    residual = target - operate(iterate)
    local_sum = restrict(coarse_width, residual, coarse_index, weights)
    gathered_res = lax.psum(local_sum, ("grp", "dev"))
    halfway = jnp.dot(chol_inverse, gathered_res, precision=PRECISE)
    partial_terms = jnp.dot(halfway, chol_inverse, precision=PRECISE)
    correction = lax.psum(partial_terms, "dev")
    iterate = iterate + prolong(correction, coarse_index, weights)
    for sweep_index in range(POST):
        iterate = iterate + DAMPING * (target - operate(iterate)) / diag_total
    return iterate[None, None]


def solution(mesh):
    return jax.shard_map(
        local,
        mesh=mesh,
        in_specs=(
            P("grp", "dev", None, None),
            P("grp", "dev", None, None),
            P("grp", "dev", None),
            P("grp", "dev", None, None),
            P("grp", "dev", None, None),
            P("grp", "dev", None, None),
            P("grp", "dev", None, None),
            P(),
            P("dev", None),
        ),
        out_specs=P("grp", "dev", None, None),
        check_vma=False,
    )
```

profile of v0, /device:TPU:0, one launch (start us, length us, event | category | flops | bytes accessed | tf_op | source)
XLA Modules:
  0.0 980.4 jit_solution(13841253639486195369)
XLA Ops:
  11.6 74.9 %scatter_fusion = f32[3,4096]{0,1:T(8,128)S(1)} fusion(f32[3,4096]{0,1:T(8,128)S(1)} %copy-done.3, s32[13824]{0:T(1024)S(1)} %reshape.222, f32[13824,3]{1,0:T(8,128)} %bitcast.211), kind=kCustom, calls=%fused_computation.11 | custom fusion | flops 41472 | bytes 552960 | tf_op jit(solution)/shard_map/scatter-add | solution.py:81
  86.4 7.6 gather_fusion.1
  109.3 13.6 %scatter_fusion.1 = f32[3,4096]{0,1:T(8,128)} fusion(f32[3,4096]{0,1:T(8,128)} %copy-done.4, s32[2048]{0:T(1024)S(1)} %bitcast.231, f32[2048,3]{1,0:T(8,128)} %bitcast.213), kind=kCustom, calls=%fused_computation.12 | custom fusion | flops 6144 | bytes 81920 | tf_op jit(solution)/shard_map/scatter-add | solution.py:34
  127.6 27.7 %gather_fusion.2 = f32[13824,3]{1,0:T(8,128)} fusion(f32[3,4096]{0,1:T(8,128)} %get-tuple-element.11, s32[14336]{0:T(1024)S(1)} %pad_clamp_fusion), kind=kCustom, calls=%fused_computation.2 | custom fusion | bytes 387072 | tf_op jit(solution)/shard_map/gather | solution.py:21
  164.8 69.5 %scatter_fusion.2 = f32[3,4096]{0,1:T(8,128)} fusion(f32[3,4096]{0,1:T(8,128)} %get-tuple-element.12, s32[13824]{0:T(1024)S(1)} %reshape.222, f32[13824,3]{1,0:T(8,128)} %bitcast.204), kind=kCustom, calls=%fused_computation.13 | custom fusion | flops 41472 | bytes 552960 | tf_op jit(solution)/shard_map/scatter-add | solution.py:23
  234.4 9.2 gather_fusion.3
  259.5 13.6 %scatter_fusion.3 = f32[3,4096]{0,1:T(8,128)} fusion(f32[3,4096]{0,1:T(8,128)} %scatter_fusion.2, s32[2048]{0:T(1024)S(1)} %bitcast.232, f32[2048,3]{1,0:T(8,128)} %bitcast.214), kind=kCustom, calls=%fused_computation.14 | custom fusion | flops 6144 | bytes 81920 | tf_op jit(solution)/shard_map/scatter-add | solution.py:34
  278.7 27.7 %gather_fusion.4 = f32[13824,3]{1,0:T(8,128)} fusion(f32[3,4096]{0,1:T(8,128)} %get-tuple-element.10, s32[14336]{0:T(1024)S(1)} %pad_clamp_fusion), kind=kCustom, calls=%fused_computation.4 | custom fusion | bytes 387072 | tf_op jit(solution)/shard_map/gather | solution.py:21
  315.9 69.6 %scatter_fusion.4 = f32[3,4096]{0,1:T(8,128)} fusion(f32[3,4096]{0,1:T(8,128)} %get-tuple-element.9, s32[13824]{0:T(1024)S(1)} %reshape.222, f32[13824,3]{1,0:T(8,128)} %bitcast.205), kind=kCustom, calls=%fused_computation.15 | custom fusion | flops 41472 | bytes 552960 | tf_op jit(solution)/shard_map/scatter-add | solution.py:23
  385.5 9.1 gather_fusion.5
  410.8 13.7 %scatter_fusion.5 = f32[3,4096]{0,1:T(8,128)} fusion(f32[3,4096]{0,1:T(8,128)} %scatter_fusion.4, s32[2048]{0:T(1024)S(1)} %bitcast.233, f32[2048,3]{1,0:T(8,128)} %bitcast.215), kind=kCustom, calls=%fused_computation.16 | custom fusion | flops 6144 | bytes 81920 | tf_op jit(solution)/shard_map/scatter-add | solution.py:34
  431.6 87.8 %scatter_custom_fusion.6 = f32[3,1536]{0,1:T(8,128)S(1)} fusion(s32[16384]{0:T(1024)S(1)} %bitcast.239, f32[16384,3]{1,0:T(8,128)} %bitcast.202, f32[]{:T(128)} %constant.10.clone.1), kind=kCustom, calls=%fused_computation.52 | custom fusion | flops 49152 | bytes 18944 | tf_op jit(solution)/shard_map/scatter-add | solution.py:42
  519.7 43.6 %psum.14 = f32[4608]{0:T(1024)S(1)} all-reduce(f32[4608]{0:T(1024)S(1)} %reshape.128), channel_id=1, replica_groups=mesh['grp'=8,'dev'=4] {'grp','dev'}, use_global_device_ids=true, to_apply=%region_7.8 | all-reduce | flops 4608 | bytes 36864 | tf_op jit(solution)/shard_map/psum | solution.py:89
  563.4 20.3 %convolution_bitcast_fusion = f32[1152,1]{0,1:T(1,128)S(1)} fusion(f32[4608,1]{0,1:T(1,128)S(1)} %reshape.329, f32[1152,4608]{1,0:T(8,128)} %param.17), kind=kOutput, calls=%fused_computation.25 | convolution fusion | flops 63700992 | bytes 21256704 | tf_op jit(solution)/shard_map/dot_general | solution.py:90
  583.7 14.0 %convolution_reduce_fusion = f32[4608]{0:T(1024)S(1)} fusion(f32[1152,1]{0,1:T(1,128)S(1)} %convolution_bitcast_fusion, f32[1152,4608]{1,0:T(8,128)} %param.17), kind=kOutput, calls=%fused_computation.51 | convolution fusion | flops 63700992 | bytes 21256704 | tf_op jit(solution)/shard_map/dot_general | solution.py:91
  598.9 20.5 %psum.15 = f32[3,1536]{0,1:T(8,128)S(1)} all-reduce(f32[3,1536]{0,1:T(8,128)} %copy.57), channel_id=1, replica_groups=mesh['grp'=8,'dev'=4] {'dev'}, use_global_device_ids=true, to_apply=%region_8.9 | all-reduce | flops 4608 | bytes 36864 | tf_op jit(solution)/shard_map/psum | solution.py:92
  619.4 54.4 %gather_fusion.6 = f32[16384,3]{1,0:T(8,128)} fusion(f32[3,1536]{0,1:T(8,128)S(1)} %psum.15, s32[16384]{0:T(1024)S(1)} %broadcast_clamp_fusion), kind=kCustom, calls=%fused_computation.6 | custom fusion | bytes 458752 | tf_op jit(solution)/shard_map/gather | solution.py:49
  681.6 27.7 %gather_fusion.7 = f32[13824,3]{1,0:T(8,128)} fusion(f32[3,4096]{0,1:T(8,128)} %get-tuple-element.8, s32[14336]{0:T(1024)S(1)} %pad_clamp_fusion), kind=kCustom, calls=%fused_computation.7 | custom fusion | bytes 387072 | tf_op jit(solution)/shard_map/gather | solution.py:21
  718.8 69.5 %scatter_fusion.6 = f32[3,4096]{0,1:T(8,128)} fusion(f32[3,4096]{0,1:T(8,128)} %get-tuple-element.7, s32[13824]{0:T(1024)S(1)} %reshape.222, f32[13824,3]{1,0:T(8,128)} %bitcast.206), kind=kCustom, calls=%fused_computation.18 | custom fusion | flops 41472 | bytes 552960 | tf_op jit(solution)/shard_map/scatter-add | solution.py:23
  788.3 9.2 gather_fusion.8
  811.4 13.6 %scatter_fusion.7 = f32[3,4096]{0,1:T(8,128)} fusion(f32[3,4096]{0,1:T(8,128)} %scatter_fusion.6, s32[2048]{0:T(1024)S(1)} %bitcast.234, f32[2048,3]{1,0:T(8,128)} %bitcast.216), kind=kCustom, calls=%fused_computation.19 | custom fusion | flops 6144 | bytes 81920 | tf_op jit(solution)/shard_map/scatter-add | solution.py:34
  831.2 27.7 %gather_fusion.9 = f32[13824,3]{1,0:T(8,128)} fusion(f32[3,4096]{0,1:T(8,128)} %get-tuple-element.6, s32[14336]{0:T(1024)S(1)} %pad_clamp_fusion), kind=kCustom, calls=%fused_computation.9 | custom fusion | bytes 387072 | tf_op jit(solution)/shard_map/gather | solution.py:21
  868.5 69.6 %scatter_fusion.8 = f32[3,4096]{0,1:T(8,128)} fusion(f32[3,4096]{0,1:T(8,128)} %get-tuple-element.5, s32[13824]{0:T(1024)S(1)} %reshape.222, f32[13824,3]{1,0:T(8,128)} %bitcast.203), kind=kCustom, calls=%fused_computation.20 | custom fusion | flops 41472 | bytes 552960 | tf_op jit(solution)/shard_map/scatter-add | solution.py:23
  959.1 13.3 %scatter_fusion.9 = f32[3,4096]{0,1:T(8,128)} fusion(f32[3,4096]{0,1:T(8,128)} %scatter_fusion.8, s32[2048]{0:T(1024)S(1)} %bitcast.235, f32[2048,3]{1,0:T(8,128)S(1)} %bitcast.212), kind=kCustom, calls=%fused_computation.21 | custom fusion | flops 6144 | bytes 81920 | tf_op jit(solution)/shard_map/scatter-add | solution.py:34
  (158 shorter events, 172.0 us)
Async XLA Ops:
  11.5 93.1 %copy-start.9 = (f32[1,1,3,4096]{3,1,2,0:T(1,128)S(1)}, f32[1,1,3,4096]{3,1,2,0:T(1,128)}, u32[]{:S(2)}) copy-start(f32[1,1,3,4096]{3,1,2,0:T(1,128)} %param.9) | copy-start | bytes 147460
  86.4 18.2 %copy-start.4 = (f32[3,4096]{0,1:T(8,128)}, f32[3,4096]{0,1:T(8,128)S(1)}, u32[]{:S(2)}) copy-start(f32[3,4096]{0,1:T(8,128)S(1)} %scatter_fusion) | copy-start | bytes 147460
  95.6 9.7 collective-permute-start
  100.5 5.5 collective-permute-start.1
  101.8 4.3 collective-permute-start.2
  103.3 4.6 collective-permute-start.3
  164.8 92.0 %copy-start.7 = (s32[1,1,4,4096]{3,2,1,0:T(4,128)S(1)}, s32[1,1,4,4096]{3,2,1,0:T(4,128)}, u32[]{:S(2)}) copy-start(s32[1,1,4,4096]{3,2,1,0:T(4,128)} %param.14) | copy-start | bytes 196612
  245.1 11.7 %collective-permute-start.4 = (f32[3,512]{1,0:T(4,128)S(1)}, f32[3,512]{1,0:T(4,128)S(1)}, u32[]{:S(2)}, u32[]{:S(2)}) collective-permute-start(f32[3,512]{1,0:T(4,128)S(1)} %get-tuple-element.25), channel_id=1, source_target_pairs={{0,4},{4,8},{8,12},{12,16},{16,20},{20,24},{24,28},{1,5},{5,9},{9,... | collective-permute-start | bytes 18440 | tf_op jit(solution)/shard_map/ppermute | solution.py:16
  249.7 7.2 collective-permute-start.5
  251.0 5.9 collective-permute-start.6
  255.0 3.1 collective-permute-start.7
  396.2 11.4 %collective-permute-start.8 = (f32[3,512]{1,0:T(4,128)S(1)}, f32[3,512]{1,0:T(4,128)S(1)}, u32[]{:S(2)}, u32[]{:S(2)}) collective-permute-start(f32[3,512]{1,0:T(4,128)S(1)} %get-tuple-element.21), channel_id=1, source_target_pairs={{0,4},{4,8},{8,12},{12,16},{16,20},{20,24},{24,28},{1,5},{5,9},{9,... | collective-permute-start | bytes 18440 | tf_op jit(solution)/shard_map/ppermute | solution.py:16
  401.2 6.5 collective-permute-start.9
  402.5 5.2 collective-permute-start.10
  406.4 3.1 collective-permute-start.11
  673.8 5.5 copy-start.5
  799.1 8.0 collective-permute-start.12
  803.0 5.5 collective-permute-start.13
  804.3 4.3 collective-permute-start.14
  805.8 4.1 collective-permute-start.15
  945.5 11.4 %collective-permute-start.16 = (f32[3,512]{1,0:T(4,128)S(1)}, f32[3,512]{1,0:T(4,128)S(1)}, u32[]{:S(2)}, u32[]{:S(2)}) collective-permute-start(f32[3,512]{1,0:T(4,128)S(1)} %get-tuple-element.13), channel_id=1, source_target_pairs={{0,4},{4,8},{8,12},{12,16},{16,20},{20,24},{24,28},{1,5},{5,9},{9,... | collective-permute-start | bytes 18440 | tf_op jit(solution)/shard_map/ppermute | solution.py:16
  950.0 6.9 collective-permute-start.17
  951.3 5.6 collective-permute-start.18
  955.6 3.1 collective-permute-start.19
  (6 other events, 17.7 us)
where the time goes:
time: 993 us; the launch traced here: 980 us
  other arithmetic  551 us (55%)
  local copies, waits for them, and re-layouts  267 us (27%)
  blocking collectives  64.2 us (6%)
  starting transfers between devices  51.3 us (5%)
  matrix products  35.6 us (4%)
    scatter-add x4, other arithmetic, element_apply(): jnp.zeros_like(field).at[:, node_index]  278 us
    gather x8, local copies, waits for them, and re-layouts, element_apply(): gathered = field[:, node_index].reshape(81, elem_count)  131 us
    scatter-add x1, other arithmetic, restrict(): return jnp.zeros((3, coarse_width), field.dtype).at[:, coarse_index].add(...  87.8 us
    scatter-add x1, other arithmetic, local(): local_diag = jnp.zeros_like(mass_here).at[:, node_index].add(main_diag[:,...  74.9 us
    scatter-add x5, other arithmetic, exchange_faces(): return field.at[:, face_index].add(received, mode='drop')  67.7 us
    gather x1, local copies, waits for them, and re-layouts, prolong(): return jnp.sum(weights[None] * coarse_table[:, coarse_index], axis=1)  54.4 us
    ppermute x20, starting transfers between devices, from_behind(): lax.ppermute(value, axis, [(source, source + steps) for source in range(i...  51.3 us
    gather x10, local copies, waits for them, and re-layouts, exchange_faces(): outgoing = field.at[:, face_index].get(mode='fill', fill_value=0.0)  48.6 us
  transfers between devices with their start and end apart: 20, of which 7 were waited for; matrix products, arithmetic and copies ran while one was open for 0% of the time, Pallas kernels for 0%

commit v1 on v0

v1 whole, which is shorter than its diff:
```python
import jax
import jax.numpy as jnp
from jax import lax
from jax.experimental import pallas as pl
from jax.experimental.pallas import tpu as pltpu
from jax.sharding import PartitionSpec as P

POST = 2
DAMPING = 0.6
WINDOW = 64
LANES = 128
F32 = jnp.float32
BF16 = jnp.bfloat16


def two_parts(value):
    high = value.astype(BF16)
    low = (value - high.astype(F32)).astype(BF16)
    return high, low


def nt_dot(left, right):
    return lax.dot_general(left, right, (((1,), (1,)), ((), ())), preferred_element_type=F32)


def low_onehot(index_row):
    low = index_row & (LANES - 1)
    rows = lax.broadcasted_iota(jnp.int32, (LANES, index_row.shape[1]), 0)
    return jnp.where(rows == low, 1.0, 0.0).astype(BF16)


def high_mask(index_row, count):
    rows = lax.broadcasted_iota(jnp.int32, (count, index_row.shape[1]), 0)
    return rows == (index_row >> 7)


def field_parts(field):
    high, low = two_parts(field)
    return jnp.concatenate([high, low], axis=1)


def gather_slot(parts, index_row):
    count = parts.shape[0] // 3
    onehot = low_onehot(index_row)
    picked = jnp.dot(parts, jnp.concatenate([onehot, onehot], axis=0), preferred_element_type=F32)
    mask = high_mask(index_row, count)
    return [
        jnp.sum(jnp.where(mask, picked[c * count:(c + 1) * count], 0.0), axis=0, keepdims=True)
        for c in range(3)
    ]


def scatter_slot(rows_high, rows_low, index_row, count):
    mask = high_mask(index_row, count)
    spread = [
        jnp.where(mask, row, 0.0).astype(BF16)
        for row in rows_high + rows_low
    ]
    return nt_dot(jnp.concatenate(spread, axis=0), low_onehot(index_row))


def join_parts(total):
    half = total.shape[0] // 2
    return total[:half] + total[half:]


def slot_rows(par_ref):
    grp_odd = par_ref[0]
    dev_odd = par_ref[1]
    return [1 - grp_odd, grp_odd, 3 - dev_odd, 2 + dev_odd]


def send_faces(field, faces_ref, par_ref, out_refs):
    parts = field_parts(field)
    for slot, face in enumerate(slot_rows(par_ref)):
        rows = gather_slot(parts, faces_ref[pl.ds(face, 1), :])
        out_refs[slot][...] = jnp.concatenate(rows, axis=0)


def add_faces(faces_ref, par_ref, in_refs, count):
    total = None
    for slot, face in enumerate(slot_rows(par_ref)):
        value = in_refs[slot][...]
        high = value.astype(BF16).astype(F32)
        low = value - high
        got = scatter_slot(
            [high[c:c + 1] for c in range(3)],
            [low[c:c + 1] for c in range(3)],
            faces_ref[pl.ds(face, 1), :],
            count,
        )
        total = got if total is None else total + got
    return join_parts(total)


def scatter_elements(high_ref, low_ref, nodes_ref, count):
    local = nodes_ref.shape[0]
    total = None
    for i in range(local):
        got = scatter_slot(
            [high_ref[c * local + i:c * local + i + 1, :] for c in range(3)],
            [low_ref[c * local + i:c * local + i + 1, :] for c in range(3)],
            nodes_ref[i:i + 1, :],
            count,
        )
        total = got if total is None else total + got
    return join_parts(total)


def store_parts(value, high_ref, low_ref):
    high = value.astype(BF16).astype(F32)
    high_ref[...] = high
    low_ref[...] = value - high


def element_apply(field, nodes_ref, coef_ref, matrix_ref, mat_s, got_s, high_s, low_s):
    count = field.shape[0] // 3
    local = nodes_ref.shape[0]
    size = matrix_ref.shape[0]
    mat_s[...] = jnp.zeros_like(mat_s)
    mat_s[:size, :size] = matrix_ref[...]
    parts = field_parts(field)
    got_s[80:, :] = jnp.zeros_like(got_s[80:, :])
    for i in range(local):
        rows = gather_slot(parts, nodes_ref[i:i + 1, :])
        for c in range(3):
            got_s[c * local + i:c * local + i + 1, :] = rows[c]
    mat_high, mat_low = two_parts(mat_s[...])
    got_high, got_low = two_parts(got_s[...])
    product = (
        jnp.dot(mat_high, got_high, preferred_element_type=F32)
        + jnp.dot(mat_high, got_low, preferred_element_type=F32)
        + jnp.dot(mat_low, got_high, preferred_element_type=F32)
    )
    store_parts(product * coef_ref[...], high_s, low_s)
    return scatter_elements(high_s, low_s, nodes_ref, count)


def diag_kernel(par, nodes, coef, mass, faces, matrix, diag_out, s0, s1, s2, s3, high_s, low_s):
    size = matrix.shape[0]
    rows = lax.broadcasted_iota(jnp.int32, (size, size), 0)
    cols = lax.broadcasted_iota(jnp.int32, (size, size), 1)
    main = jnp.sum(jnp.where(rows == cols, matrix[...], 0.0), axis=1, keepdims=True)
    value = main * coef[...]
    high = value.astype(BF16).astype(F32)
    high_s[:size, :] = high
    low_s[:size, :] = value - high
    diag = mass[...] + scatter_elements(high_s, low_s, nodes, mass.shape[0] // 3)
    diag_out[...] = diag
    send_faces(diag, faces, par, (s0, s1, s2, s3))


def first_kernel(par, diag, g0, g1, g2, g3, right, nodes, coef, mass, faces, matrix,
                 gain_out, field_out, local_out, s0, s1, s2, s3, mat_s, got_s, high_s, low_s):
    count = mass.shape[0] // 3
    total = diag[...] + add_faces(faces, par, (g0, g1, g2, g3), count)
    gain = DAMPING / total
    gain_out[...] = gain
    field = gain * right[...]
    field_out[...] = field
    local = mass[...] * field + element_apply(field, nodes, coef, matrix, mat_s, got_s, high_s, low_s)
    local_out[...] = local
    send_faces(local, faces, par, (s0, s1, s2, s3))


def sweep_kernel(par, local_in, g0, g1, g2, g3, field_in, gain, right, nodes, coef, mass, faces, matrix,
                 field_out, local_out, s0, s1, s2, s3, mat_s, got_s, high_s, low_s):
    count = mass.shape[0] // 3
    total = local_in[...] + add_faces(faces, par, (g0, g1, g2, g3), count)
    field = field_in[...] + gain[...] * (right[...] - total)
    field_out[...] = field
    local = mass[...] * field + element_apply(field, nodes, coef, matrix, mat_s, got_s, high_s, low_s)
    local_out[...] = local
    send_faces(local, faces, par, (s0, s1, s2, s3))


def last_kernel(par, local_in, g0, g1, g2, g3, field_in, gain, right, faces, field_out):
    count = right.shape[0] // 3
    total = local_in[...] + add_faces(faces, par, (g0, g1, g2, g3), count)
    field_out[...] = field_in[...] + gain[...] * (right[...] - total)


def transfer_matrix(home, width, coarse, weights):
    total = None
    for q in range(coarse.shape[0]):
        offset = coarse[q:q + 1, :] - home
        offset = jnp.where(offset < 0, offset + width, offset)
        rows = lax.broadcasted_iota(jnp.int32, (WINDOW, coarse.shape[1]), 0)
        part = jnp.where(rows == offset, weights[q:q + 1, :], 0.0)
        total = part if total is None else total + part
    return total


def prepare_kernel(width, par, coarse, weights, high_out, low_out):
    high, low = two_parts(transfer_matrix(par[2], width, coarse, weights))
    high_out[...] = high
    low_out[...] = low


def restrict_kernel(par, local_in, g0, g1, g2, g3, right, faces, high_in, low_in, out, res_s, flat_s):
    count = right.shape[0] // 3
    total = local_in[...] + add_faces(faces, par, (g0, g1, g2, g3), count)
    res_s[...] = right[...] - total
    flat_s[...] = jnp.zeros_like(flat_s)
    for h in range(count):
        for c in range(3):
            flat_s[c:c + 1, h * LANES:(h + 1) * LANES] = res_s[c * count + h:c * count + h + 1, :]
    high, low = two_parts(flat_s[...])
    out[...] = nt_dot(high, high_in[...]) + nt_dot(low, high_in[...]) + nt_dot(high, low_in[...])


def prolong_kernel(par, window, field_in, nodes, coef, mass, faces, matrix, high_in, low_in,
                   field_out, local_out, s0, s1, s2, s3, mat_s, got_s, high_s, low_s, flat_s, res_s):
    count = mass.shape[0] // 3
    high, low = two_parts(window[...])
    flat_s[...] = (
        jnp.dot(high, high_in[...], preferred_element_type=F32)
        + jnp.dot(low, high_in[...], preferred_element_type=F32)
        + jnp.dot(high, low_in[...], preferred_element_type=F32)
    )
    for h in range(count):
        for c in range(3):
            res_s[c * count + h:c * count + h + 1, :] = flat_s[c:c + 1, h * LANES:(h + 1) * LANES]
    field = field_in[...] + res_s[...]
    field_out[...] = field
    local = mass[...] * field + element_apply(field, nodes, coef, matrix, mat_s, got_s, high_s, low_s)
    local_out[...] = local
    send_faces(local, faces, par, (s0, s1, s2, s3))


def coarse_kernel(rhs, factor, out):
    @pl.when(pl.program_id(0) == 0)
    def _():
        out[...] = jnp.zeros_like(out)

    block = factor[...]
    half = jnp.sum(block * rhs[...], axis=1, keepdims=True)
    out[...] += jnp.sum(block * half, axis=0, keepdims=True)


def local_program(mesh_shape, right_side, elem_nodes, elem_coef, node_mass, face_slots, coarse_nodes,
                  coarse_weights, elem_matrix, chol_inverse):
    n_grp, n_dev = mesh_shape
    nodes_count = right_side.shape[-1]
    hi = nodes_count // LANES
    local_nodes, elements = elem_nodes.shape[2:]
    slots = face_slots.shape[-1]
    width = chol_inverse.shape[1] // 3
    stride = width // (n_grp * n_dev)
    grp = lax.axis_index("grp")
    dev = lax.axis_index("dev")
    home = (grp * n_dev + dev) * width // (n_grp * n_dev)
    par = jnp.stack([grp & 1, dev & 1, home, dev]).astype(jnp.int32)

    right = right_side.reshape(3 * hi, LANES)
    mass = node_mass.reshape(3 * hi, LANES)
    nodes = elem_nodes[0, 0]
    coef = elem_coef[0]
    faces = face_slots[0, 0]
    coarse = coarse_nodes[0, 0]
    weights = coarse_weights[0, 0]

    smem = pl.BlockSpec(memory_space=pltpu.SMEM)
    vmem = pl.BlockSpec(memory_space=pltpu.VMEM)
    field_t = jax.ShapeDtypeStruct((3 * hi, LANES), F32)
    face_t = [jax.ShapeDtypeStruct((3, slots), F32)] * 4
    rows = 3 * local_nodes
    padded = -(-rows // LANES) * LANES
    part_rows = -(-rows // 16) * 16
    parts_s = [pltpu.VMEM((part_rows, elements), F32)] * 2
    apply_s = [pltpu.VMEM((part_rows, padded), F32), pltpu.VMEM((padded, elements), F32)] + parts_s
    flat_s = pltpu.VMEM((8, nodes_count), F32)

    def call(kernel, outs, scratch, *args):
        return pl.pallas_call(
            kernel,
            out_shape=outs,
            in_specs=[smem] + [vmem] * (len(args) - 1),
            out_specs=jax.tree.map(lambda _: vmem, outs),
            scratch_shapes=scratch,
        )(*args)

    def pairs(axis, parity):
        count = lax.axis_size(axis)
        out = []
        for first in range(parity, count + parity, 2):
            a, b = first % count, (first + 1) % count
            out += [(a, b), (b, a)]
        return out

    def swap(faces_out):
        return [
            lax.ppermute(faces_out[0], "grp", pairs("grp", 0)),
            lax.ppermute(faces_out[1], "grp", pairs("grp", 1)),
            lax.ppermute(faces_out[2], "dev", pairs("dev", 0)),
            lax.ppermute(faces_out[3], "dev", pairs("dev", 1)),
        ]

    transfer_t = jax.ShapeDtypeStruct((WINDOW, nodes_count), BF16)

    def prepare(*refs):
        prepare_kernel(width, *refs)

    high_t, low_t = call(prepare, [transfer_t] * 2, [], par, coarse, weights)
    diag, *out = call(diag_kernel, [field_t] + face_t, parts_s, par, nodes, coef, mass, faces, elem_matrix)
    got = swap(out)
    gain, field, local, *out = call(
        first_kernel, [field_t] * 3 + face_t, apply_s,
        par, diag, *got, right, nodes, coef, mass, faces, elem_matrix)
    got = swap(out)
    field, local, *out = call(
        sweep_kernel, [field_t] * 2 + face_t, apply_s,
        par, local, *got, field, gain, right, nodes, coef, mass, faces, elem_matrix)
    got = swap(out)
    window = call(
        restrict_kernel, jax.ShapeDtypeStruct((8, WINDOW), F32), [pltpu.VMEM((3 * hi, LANES), F32), flat_s],
        par, local, *got, right, faces, high_t, low_t)

    total = n_grp * n_dev
    sent = jnp.broadcast_to(window[None, :3], (total, 3, WINDOW))
    windows = lax.all_to_all(sent, ("grp", "dev"), 0, 0)
    pieces = jnp.zeros((total, 3, stride), F32)
    for step in range(-(-WINDOW // stride)):
        piece = windows[:, :, step * stride:(step + 1) * stride]
        piece = jnp.pad(piece, ((0, 0), (0, 0), (0, stride - piece.shape[2])))
        pieces = pieces + jnp.roll(piece, step, axis=0)
    rhs = pieces.transpose(1, 0, 2).reshape(1, 3 * width)

    block = chol_inverse.shape[0]
    while block % 16 == 0 and block > 144:
        block //= 2
    part = pl.pallas_call(
        coarse_kernel,
        grid=(chol_inverse.shape[0] // block,),
        out_shape=jax.ShapeDtypeStruct((1, 3 * width), F32),
        in_specs=[
            pl.BlockSpec((1, 3 * width), lambda i: (0, 0)),
            pl.BlockSpec((block, 3 * width), lambda i: (i, 0)),
        ],
        out_specs=pl.BlockSpec((1, 3 * width), lambda i: (0, 0)),
    )(rhs, chol_inverse)
    table = part.reshape(3, width)
    table = jnp.concatenate([table, table[:, :n_dev * stride + WINDOW]], axis=1)

    def window_of(other):
        return lax.dynamic_slice(table, (0, (grp * n_dev + other) * stride), (3, WINDOW))

    correction = window_of(dev)
    for step in range(1, n_dev):
        correction = correction + lax.ppermute(
            window_of(dev ^ step), "dev", [(i, i ^ step) for i in range(n_dev)])
    correction = jnp.pad(correction, ((0, 5), (0, 0)))

    field, local, *out = call(
        prolong_kernel, [field_t] * 2 + face_t, apply_s + [flat_s, pltpu.VMEM((3 * hi, LANES), F32)],
        par, correction, field, nodes, coef, mass, faces, elem_matrix, high_t, low_t)
    for _ in range(POST - 1):
        got = swap(out)
        field, local, *out = call(
            sweep_kernel, [field_t] * 2 + face_t, apply_s,
            par, local, *got, field, gain, right, nodes, coef, mass, faces, elem_matrix)
    got = swap(out)
    field = call(last_kernel, field_t, [], par, local, *got, field, gain, right, faces)
    return field.reshape(1, 1, 3, nodes_count)


def solution(mesh):
    mesh_shape = (mesh.shape["grp"], mesh.shape["dev"])

    def local(*args):
        return local_program(mesh_shape, *args)

    return jax.shard_map(
        local,
        mesh=mesh,
        in_specs=(
            P("grp", "dev", None, None),
            P("grp", "dev", None, None),
            P("grp", "dev", None),
            P("grp", "dev", None, None),
            P("grp", "dev", None, None),
            P("grp", "dev", None, None),
            P("grp", "dev", None, None),
            P(),
            P("dev", None),
        ),
        out_specs=P("grp", "dev", None, None),
        check_vma=False,
    )
```

time: 993 us -> 109 us (0.11); the launches traced: 980 us -> 109 us
  other arithmetic: 551 us -> 2.29 us
  local copies, waits for them, and re-layouts: 267 us -> 7.83 us
  blocking collectives: 64.2 us -> 0 us
  Pallas kernels: 0 us -> 48.6 us
  matrix products: 35.6 us -> 0 us
  starting transfers between devices: 51.3 us -> 30.3 us
    scatter-add x11 -> x0, other arithmetic: 509 us -> none  [the longest x4 278 us: element_apply(): jnp.zeros_like(field).at[:, node_index]]
    gather x20 -> x0, local copies, waits for them, and re-layouts: 235 us -> none  [the longest x8 131 us: element_apply(): gathered = field[:, node_index].reshape(81, elem_count)]
    psum x2 -> x0, blocking collectives: 64.2 us -> none  [the longest x1 43.6 us: local(): gathered_res = lax.psum(local_sum, ('grp', 'dev'))]
    pallas_call x0 -> x9, Pallas kernels: none -> 48.6 us  [the longest x8 37.5 us: call(): pl.pallas_call(kernel, out_shape=outs, in_specs=[smem] + [vmem] * (len(ar...]
    dot_general x6 -> x0, matrix products: 35.6 us -> none  [the longest x1 20.3 us: local(): halfway = jnp.dot(chol_inverse, gathered_res, precision=PRECISE)]
    ppermute x20 -> x23, starting transfers between devices: 51.3 us -> 26.7 us  [the longest x5 13.1 us: swap(): lax.ppermute(faces_out[1], 'grp', pairs('grp', 1))]
    mul x5 -> x0, other arithmetic: 23 us -> none  [the longest x3 14.2 us: element_apply(): return summed + mass_here * field]
    reshape x15 -> x2, local copies, waits for them, and re-layouts: 18.1 us -> 0.72 us  [the longest x1 0.7 us: local_program(): rhs = pieces.transpose(1, 0, 2).reshape(1, 3 * width)]
  transfers between devices with their start and end apart: 20 -> 24, of which waited for: 7 -> 9; matrix products, arithmetic and copies ran while one was open for 0% -> 0% of each run, Pallas kernels for 0% -> 2%
where the time goes in v1:
time: 109 us
  Pallas kernels  48.6 us (45%)
  starting transfers between devices  30.3 us (28%)
  waiting for transfers between devices  19.6 us (18%)
  local copies, waits for them, and re-layouts  7.83 us (7%)
  other arithmetic  2.29 us (2%)
    pallas_call x8, Pallas kernels, call(): pl.pallas_call(kernel, out_shape=outs, in_specs=[smem] + [vmem] * (len(ar...  37.5 us
    ppermute x5, starting transfers between devices, swap(): lax.ppermute(faces_out[1], 'grp', pairs('grp', 1))  13.1 us
    pallas_call x1, Pallas kernels, local_program(): pl.pallas_call(coarse_kernel, grid=(chol_inverse.shape[0] // block,), out...  11 us
    ppermute x5, waiting for transfers between devices, swap(): lax.ppermute(faces_out[1], 'grp', pairs('grp', 1))  9.13 us
    ppermute x5, starting transfers between devices, swap(): lax.ppermute(faces_out[3], 'dev', pairs('dev', 1))  7.68 us
    all_to_all x1, waiting for transfers between devices, local_program(): windows = lax.all_to_all(sent, ('grp', 'dev'), 0, 0)  7.23 us
    unnamed x43, local copies, waits for them, and re-layouts  5.18 us
    ppermute x5, starting transfers between devices, swap(): lax.ppermute(faces_out[0], 'grp', pairs('grp', 0))  3.75 us
  transfers between devices with their start and end apart: 24, of which 9 were waited for; matrix products, arithmetic and copies ran while one was open for 0% of the time, Pallas kernels for 2%

profile of v1, /device:TPU:0, one launch (start us, length us, event | category | flops | bytes accessed | tf_op | source)
XLA Modules:
  0.0 108.7 jit_solution(8465553553282579362)
XLA Ops:
  2.1 3.4 %shard_map.91 = (f32[96,128]{1,0:T(8,128)}, f32[3,512]{1,0:T(4,128)}, f32[3,512]{1,0:T(4,128)}, f32[3,512]{1,0:T(4,128)}, f32[3,512]{1,0:T(4,128)}) custom-call(s32[4]{0:T(128)} %pad_add_fusion.par.refs_0_, s32[27,512]{1,0:T(8,128)} %bitcast.16, f32[1,512]{1,0:T(1,128)} %bitcast.40, f32[96,128]{1,0:T(8,128)} %bitcast.26, s32[4,512]{1,0:T(4,128)} %bitcast.31, ...), custom_call_target="tpu_custom_call" | custom-call | tf_op jit(solution)/shard_map/pallas_call | solution.py:275
  5.5 3.0 %collective-permute-start = (f32[3,512]{1,0:T(4,128)}, f32[3,512]{1,0:T(4,128)S(1)}, u32[]{:S(2)}, u32[]{:S(2)}) collective-permute-start(f32[3,512]{1,0:T(4,128)} %get-tuple-element.38), channel_id=1, source_target_pairs={{0,4},{4,0},{8,12},{12,8},{16,20},{20,16},{24,28},{28,24},{1,5},{5... | collective-permute-start | bytes 18440 | tf_op jit(solution)/shard_map/ppermute | solution.py:293
  8.5 3.5 %collective-permute-start.1 = (f32[3,512]{1,0:T(4,128)}, f32[3,512]{1,0:T(4,128)S(1)}, u32[]{:S(2)}, u32[]{:S(2)}) collective-permute-start(f32[3,512]{1,0:T(4,128)} %get-tuple-element.39), channel_id=1, source_target_pairs={{4,8},{8,4},{12,16},{16,12},{20,24},{24,20},{28,0},{0,28},{5,9},{9... | collective-permute-start | bytes 18440 | tf_op jit(solution)/shard_map/ppermute | solution.py:294
  12.0 1.6 %collective-permute-start.3 = (f32[3,512]{1,0:T(4,128)}, f32[3,512]{1,0:T(4,128)S(1)}, u32[]{:S(2)}, u32[]{:S(2)}) collective-permute-start(f32[3,512]{1,0:T(4,128)} %get-tuple-element.41), channel_id=1, source_target_pairs={{1,2},{2,1},{3,0},{0,3},{5,6},{6,5},{7,4},{4,7},{9,10},{10,9},{11,... | collective-permute-start | bytes 18440 | tf_op jit(solution)/shard_map/ppermute | solution.py:296
  15.9 6.5 %shard_map.92 = (f32[96,128]{1,0:T(8,128)}, f32[96,128]{1,0:T(8,128)}, f32[96,128]{1,0:T(8,128)}, f32[3,512]{1,0:T(4,128)}, f32[3,512]{1,0:T(4,128)}, /*index=5*/f32[3,512]{1,0:T(4,128)}, f32[3,512]{1,0:T(4,128)}) custom-call(s32[4]{0:T(128)} %pad_add_fusion.par.refs_0_, f32[96,128]{1,0:T(8,128)} %get-tuple-element.37.diag, f32[3,512]{1,0:T(4,128)} %copy-done.5, ...), custom_call_target="tpu_custom_call" | custom-call | tf_op jit(solution)/shard_map/pallas_call | solution.py:275
  22.4 3.4 %collective-permute-start.5 = (f32[3,512]{1,0:T(4,128)}, f32[3,512]{1,0:T(4,128)S(1)}, u32[]{:S(2)}, u32[]{:S(2)}) collective-permute-start(f32[3,512]{1,0:T(4,128)} %get-tuple-element.44), channel_id=1, source_target_pairs={{4,8},{8,4},{12,16},{16,12},{20,24},{24,20},{28,0},{0,28},{5,9},{9... | collective-permute-start | bytes 18440 | tf_op jit(solution)/shard_map/ppermute | solution.py:294
  25.8 1.6 %collective-permute-start.7 = (f32[3,512]{1,0:T(4,128)}, f32[3,512]{1,0:T(4,128)S(1)}, u32[]{:S(2)}, u32[]{:S(2)}) collective-permute-start(f32[3,512]{1,0:T(4,128)} %get-tuple-element.46), channel_id=1, source_target_pairs={{1,2},{2,1},{3,0},{0,3},{5,6},{6,5},{7,4},{4,7},{9,10},{10,9},{11,... | collective-permute-start | bytes 18440 | tf_op jit(solution)/shard_map/ppermute | solution.py:296
  27.4 1.7 %collective-permute-done.5.g1 = f32[3,512]{1,0:T(4,128)S(1)} collective-permute-done((f32[3,512]{1,0:T(4,128)}, f32[3,512]{1,0:T(4,128)S(1)}, u32[]{:S(2)}, u32[]{:S(2)}) %collective-permute-start.5) | collective-permute-done | bytes 6176 | tf_op jit(solution)/shard_map/ppermute | solution.py:294
  29.7 6.5 %shard_map.93 = (f32[96,128]{1,0:T(8,128)}, f32[96,128]{1,0:T(8,128)}, f32[3,512]{1,0:T(4,128)}, f32[3,512]{1,0:T(4,128)}, f32[3,512]{1,0:T(4,128)}, /*index=5*/f32[3,512]{1,0:T(4,128)}) custom-call(s32[4]{0:T(128)} %pad_add_fusion.par.refs_0_, f32[96,128]{1,0:T(8,128)} %get-tuple-element.42.local_in, f32[3,512]{1,0:T(4,128)} %copy-done.6, ...), custom_call_target="tpu_custom_call" | custom-call | tf_op jit(solution)/shard_map/pallas_call | solution.py:275
  36.3 3.3 %collective-permute-start.9 = (f32[3,512]{1,0:T(4,128)}, f32[3,512]{1,0:T(4,128)S(1)}, u32[]{:S(2)}, u32[]{:S(2)}) collective-permute-start(f32[3,512]{1,0:T(4,128)} %get-tuple-element.51), channel_id=1, source_target_pairs={{4,8},{8,4},{12,16},{16,12},{20,24},{24,20},{28,0},{0,28},{5,9},{9... | collective-permute-start | bytes 18440 | tf_op jit(solution)/shard_map/ppermute | solution.py:294
  39.6 1.6 %collective-permute-start.11 = (f32[3,512]{1,0:T(4,128)}, f32[3,512]{1,0:T(4,128)S(1)}, u32[]{:S(2)}, u32[]{:S(2)}) collective-permute-start(f32[3,512]{1,0:T(4,128)} %get-tuple-element.53), channel_id=1, source_target_pairs={{1,2},{2,1},{3,0},{0,3},{5,6},{6,5},{7,4},{4,7},{9,10},{10,9},{11,... | collective-permute-start | bytes 18440 | tf_op jit(solution)/shard_map/ppermute | solution.py:296
  41.2 2.6 %shard_map.94 = (bf16[64,4096]{1,0:T(8,128)(2,1)}, bf16[64,4096]{1,0:T(8,128)(2,1)}) custom-call(s32[4]{0:T(128)} %pad_add_fusion.par.refs_0_, s32[4,4096]{1,0:T(4,128)} %bitcast.38, f32[4,4096]{1,0:T(4,128)} %bitcast.39), custom_call_target="tpu_custom_call" | custom-call | tf_op jit(solution)/shard_map/pallas_call | solution.py:275
  44.5 3.2 %shard_map.95 = f32[8,64]{1,0:T(8,128)} custom-call(s32[4]{0:T(128)} %pad_add_fusion.par.refs_0_, f32[96,128]{1,0:T(8,128)} %get-tuple-element.49.local_in, f32[3,512]{1,0:T(4,128)} %copy-done, f32[3,512]{1,0:T(4,128)} %copy-done.1, f32[3,512]{1,0:T(4,128)} %copy-done.2, f32[3,512]{1,0:T(4,128)} %copy-done.3, f32[96,128]{1,0:T(8,128)} %bitcast.23, ...), custom_call_target="tpu_custom_call" | custom-call | tf_op jit(solution)/shard_map/pallas_call | solution.py:275
  49.1 3.6 %all-to-all-start = ((f32[32,1,192]{2,1,0:T(1,128)}), f32[32,1,192]{2,1,0:T(1,128)S(1)}, u32[]{:S(2)}, u32[]{:S(2)}) async-start(f32[32,1,192]{2,1,0:T(1,128)} %reshape.22), calls=%async_computation | async-start | bytes 65536 | tf_op jit(solution)/shard_map/all_to_all | solution.py:321
  52.7 7.2 %all-to-all-done = f32[32,1,192]{2,1,0:T(1,128)S(1)} async-done(((f32[32,1,192]{2,1,0:T(1,128)}), f32[32,1,192]{2,1,0:T(1,128)S(1)}, u32[]{:S(2)}, u32[]{:S(2)}) %all-to-all-start) | async-done | bytes 24608 | tf_op jit(solution)/shard_map/all_to_all | solution.py:321
  62.2 11.0 %shard_map.96 = f32[1,4608]{1,0:T(1,128)} custom-call(f32[1,4608]{1,0:T(1,128)} %reshape.18.rhs, f32[1152,4608]{1,0:T(8,128)} %factor.1), custom_call_target="tpu_custom_call" | custom-call | tf_op jit(solution)/shard_map/pallas_call | solution.py:332
  76.0 1.8 %collective-permute-done.13 = f32[3,64]{1,0:T(4,128)S(1)} collective-permute-done((f32[3,64]{1,0:T(4,128)S(1)}, f32[3,64]{1,0:T(4,128)S(1)}, u32[]{:S(2)}, u32[]{:S(2)}) %collective-permute-start.13) | collective-permute-done | bytes 800 | tf_op jit(solution)/shard_map/ppermute | solution.py:350
  78.5 6.7 %shard_map.97 = (f32[96,128]{1,0:T(8,128)}, f32[96,128]{1,0:T(8,128)}, f32[3,512]{1,0:T(4,128)}, f32[3,512]{1,0:T(4,128)}, f32[3,512]{1,0:T(4,128)}, /*index=5*/f32[3,512]{1,0:T(4,128)}) custom-call(s32[4]{0:T(128)} %pad_add_fusion.par.refs_0_, f32[8,64]{1,0:T(8,128)} %pad.9.window, f32[96,128]{1,0:T(8,128)} %get-tuple-element.56.field_in, ...), custom_call_target="tpu_custom_call" | custom-call | tf_op jit(solution)/shard_map/pallas_call | solution.py:275
  87.3 1.6 %collective-permute-start.18 = (f32[3,512]{1,0:T(4,128)}, f32[3,512]{1,0:T(4,128)S(1)}, u32[]{:S(2)}, u32[]{:S(2)}) collective-permute-start(f32[3,512]{1,0:T(4,128)} %get-tuple-element.61), channel_id=1, source_target_pairs={{1,2},{2,1},{3,0},{0,3},{5,6},{6,5},{7,4},{4,7},{9,10},{10,9},{11,... | collective-permute-start | bytes 18440 | tf_op jit(solution)/shard_map/ppermute | solution.py:296
  89.1 3.3 %collective-permute-done.16.g1 = f32[3,512]{1,0:T(4,128)S(1)} collective-permute-done((f32[3,512]{1,0:T(4,128)}, f32[3,512]{1,0:T(4,128)S(1)}, u32[]{:S(2)}, u32[]{:S(2)}) %collective-permute-start.16) | collective-permute-done | bytes 6176 | tf_op jit(solution)/shard_map/ppermute | solution.py:294
  93.0 6.6 %shard_map.98 = (f32[96,128]{1,0:T(8,128)}, f32[96,128]{1,0:T(8,128)}, f32[3,512]{1,0:T(4,128)}, f32[3,512]{1,0:T(4,128)}, f32[3,512]{1,0:T(4,128)}, /*index=5*/f32[3,512]{1,0:T(4,128)}) custom-call(s32[4]{0:T(128)} %pad_add_fusion.par.refs_0_, f32[96,128]{1,0:T(8,128)} %get-tuple-element.57.local_in, f32[3,512]{1,0:T(4,128)} %copy-done.4, ...), custom_call_target="tpu_custom_call" | custom-call | tf_op jit(solution)/shard_map/pallas_call | solution.py:275
  99.6 1.5 %collective-permute-start.20 = (f32[3,512]{1,0:T(4,128)}, f32[3,512]{1,0:T(4,128)S(1)}, u32[]{:S(2)}, u32[]{:S(2)}) collective-permute-start(f32[3,512]{1,0:T(4,128)} %get-tuple-element.65), channel_id=1, source_target_pairs={{4,8},{8,4},{12,16},{16,12},{20,24},{24,20},{28,0},{0,28},{5,9},{9... | collective-permute-start | bytes 18440 | tf_op jit(solution)/shard_map/ppermute | solution.py:294
  103.4 2.8 %collective-permute-done.20.g1 = f32[3,512]{1,0:T(4,128)S(1)} collective-permute-done((f32[3,512]{1,0:T(4,128)}, f32[3,512]{1,0:T(4,128)S(1)}, u32[]{:S(2)}, u32[]{:S(2)}) %collective-permute-start.20) | collective-permute-done | bytes 6176 | tf_op jit(solution)/shard_map/ppermute | solution.py:294
  106.8 1.9 %shard_map.99 = f32[96,128]{1,0:T(8,128)} custom-call(s32[4]{0:T(128)} %pad_add_fusion.par.refs_0_, f32[96,128]{1,0:T(8,128)} %get-tuple-element.63.local_in, f32[3,512]{1,0:T(4,128)} %copy-done.10, f32[3,512]{1,0:T(4,128)} %copy-done.14, f32[3,512]{1,0:T(4,128)} %copy-done.18, f32[3,512]{1,0:T(4,128)} %copy-done.19, f32[96,128]{1,0:T(8,128)} %get-tuple-element.68.field_in, ...), custom_call_target="tpu_custom_call" | custom-call | tf_op jit(solution)/shard_map/pallas_call | solution.py:275
  (93 shorter events, 18.6 us)
Async XLA Ops:
  5.5 8.1 %collective-permute-start = (f32[3,512]{1,0:T(4,128)}, f32[3,512]{1,0:T(4,128)S(1)}, u32[]{:S(2)}, u32[]{:S(2)}) collective-permute-start(f32[3,512]{1,0:T(4,128)} %get-tuple-element.38), channel_id=1, source_target_pairs={{0,4},{4,0},{8,12},{12,8},{16,20},{20,16},{24,28},{28,24},{1,5},{5... | collective-permute-start | bytes 18440 | tf_op jit(solution)/shard_map/ppermute | solution.py:293
  8.5 6.6 %collective-permute-start.1 = (f32[3,512]{1,0:T(4,128)}, f32[3,512]{1,0:T(4,128)S(1)}, u32[]{:S(2)}, u32[]{:S(2)}) collective-permute-start(f32[3,512]{1,0:T(4,128)} %get-tuple-element.39), channel_id=1, source_target_pairs={{4,8},{8,4},{12,16},{16,12},{20,24},{24,20},{28,0},{0,28},{5,9},{9... | collective-permute-start | bytes 18440 | tf_op jit(solution)/shard_map/ppermute | solution.py:294
  12.0 3.0 %collective-permute-start.2 = (f32[3,512]{1,0:T(4,128)}, f32[3,512]{1,0:T(4,128)S(1)}, u32[]{:S(2)}, u32[]{:S(2)}) collective-permute-start(f32[3,512]{1,0:T(4,128)} %get-tuple-element.40), channel_id=1, source_target_pairs={{0,1},{1,0},{2,3},{3,2},{4,5},{5,4},{6,7},{7,6},{8,9},{9,8},{10,11... | collective-permute-start | bytes 18440 | tf_op jit(solution)/shard_map/ppermute | solution.py:295
  12.0 3.3 %collective-permute-start.3 = (f32[3,512]{1,0:T(4,128)}, f32[3,512]{1,0:T(4,128)S(1)}, u32[]{:S(2)}, u32[]{:S(2)}) collective-permute-start(f32[3,512]{1,0:T(4,128)} %get-tuple-element.41), channel_id=1, source_target_pairs={{1,2},{2,1},{3,0},{0,3},{5,6},{6,5},{7,4},{4,7},{9,10},{10,9},{11,... | collective-permute-start | bytes 18440 | tf_op jit(solution)/shard_map/ppermute | solution.py:296
  22.4 5.0 %collective-permute-start.4 = (f32[3,512]{1,0:T(4,128)}, f32[3,512]{1,0:T(4,128)S(1)}, u32[]{:S(2)}, u32[]{:S(2)}) collective-permute-start(f32[3,512]{1,0:T(4,128)} %get-tuple-element.43), channel_id=1, source_target_pairs={{0,4},{4,0},{8,12},{12,8},{16,20},{20,16},{24,28},{28,24},{1,5},{5... | collective-permute-start | bytes 18440 | tf_op jit(solution)/shard_map/ppermute | solution.py:293
  22.4 6.6 %collective-permute-start.5 = (f32[3,512]{1,0:T(4,128)}, f32[3,512]{1,0:T(4,128)S(1)}, u32[]{:S(2)}, u32[]{:S(2)}) collective-permute-start(f32[3,512]{1,0:T(4,128)} %get-tuple-element.44), channel_id=1, source_target_pairs={{4,8},{8,4},{12,16},{16,12},{20,24},{24,20},{28,0},{0,28},{5,9},{9... | collective-permute-start | bytes 18440 | tf_op jit(solution)/shard_map/ppermute | solution.py:294
  25.8 3.3 %collective-permute-start.6 = (f32[3,512]{1,0:T(4,128)}, f32[3,512]{1,0:T(4,128)S(1)}, u32[]{:S(2)}, u32[]{:S(2)}) collective-permute-start(f32[3,512]{1,0:T(4,128)} %get-tuple-element.45), channel_id=1, source_target_pairs={{0,1},{1,0},{2,3},{3,2},{4,5},{5,4},{6,7},{7,6},{8,9},{9,8},{10,11... | collective-permute-start | bytes 18440 | tf_op jit(solution)/shard_map/ppermute | solution.py:295
  25.8 3.3 %collective-permute-start.7 = (f32[3,512]{1,0:T(4,128)}, f32[3,512]{1,0:T(4,128)S(1)}, u32[]{:S(2)}, u32[]{:S(2)}) collective-permute-start(f32[3,512]{1,0:T(4,128)} %get-tuple-element.46), channel_id=1, source_target_pairs={{1,2},{2,1},{3,0},{0,3},{5,6},{6,5},{7,4},{4,7},{9,10},{10,9},{11,... | collective-permute-start | bytes 18440 | tf_op jit(solution)/shard_map/ppermute | solution.py:296
  36.2 7.7 %collective-permute-start.8 = (f32[3,512]{1,0:T(4,128)}, f32[3,512]{1,0:T(4,128)S(1)}, u32[]{:S(2)}, u32[]{:S(2)}) collective-permute-start(f32[3,512]{1,0:T(4,128)} %get-tuple-element.50), channel_id=1, source_target_pairs={{0,4},{4,0},{8,12},{12,8},{16,20},{20,16},{24,28},{28,24},{1,5},{5... | collective-permute-start | bytes 18440 | tf_op jit(solution)/shard_map/ppermute | solution.py:293
  36.3 7.5 %collective-permute-start.9 = (f32[3,512]{1,0:T(4,128)}, f32[3,512]{1,0:T(4,128)S(1)}, u32[]{:S(2)}, u32[]{:S(2)}) collective-permute-start(f32[3,512]{1,0:T(4,128)} %get-tuple-element.51), channel_id=1, source_target_pairs={{4,8},{8,4},{12,16},{16,12},{20,24},{24,20},{28,0},{0,28},{5,9},{9... | collective-permute-start | bytes 18440 | tf_op jit(solution)/shard_map/ppermute | solution.py:294
  39.6 4.2 %collective-permute-start.10 = (f32[3,512]{1,0:T(4,128)}, f32[3,512]{1,0:T(4,128)S(1)}, u32[]{:S(2)}, u32[]{:S(2)}) collective-permute-start(f32[3,512]{1,0:T(4,128)} %get-tuple-element.52), channel_id=1, source_target_pairs={{0,1},{1,0},{2,3},{3,2},{4,5},{5,4},{6,7},{7,6},{8,9},{9,8},{10,11... | collective-permute-start | bytes 18440 | tf_op jit(solution)/shard_map/ppermute | solution.py:295
  39.6 4.3 %collective-permute-start.11 = (f32[3,512]{1,0:T(4,128)}, f32[3,512]{1,0:T(4,128)S(1)}, u32[]{:S(2)}, u32[]{:S(2)}) collective-permute-start(f32[3,512]{1,0:T(4,128)} %get-tuple-element.53), channel_id=1, source_target_pairs={{1,2},{2,1},{3,0},{0,3},{5,6},{6,5},{7,4},{4,7},{9,10},{10,9},{11,... | collective-permute-start | bytes 18440 | tf_op jit(solution)/shard_map/ppermute | solution.py:296
  49.1 10.8 %all-to-all-start = ((f32[32,1,192]{2,1,0:T(1,128)}), f32[32,1,192]{2,1,0:T(1,128)S(1)}, u32[]{:S(2)}, u32[]{:S(2)}) async-start(f32[32,1,192]{2,1,0:T(1,128)} %reshape.22), calls=%async_computation | async-start | bytes 65536 | tf_op jit(solution)/shard_map/all_to_all | solution.py:321
  74.1 1.9 %collective-permute-start.12 = (f32[3,64]{1,0:T(4,128)S(1)}, f32[3,64]{1,0:T(4,128)S(1)}, u32[]{:S(2)}, u32[]{:S(2)}) collective-permute-start(f32[3,64]{1,0:T(4,128)S(1)} %get-tuple-element.69), channel_id=1, source_target_pairs={{0,1},{1,0},{2,3},{3,2},{4,5},{5,4},{6,7},{7,6},{8,9},{9,8},{10,11... | collective-permute-start | bytes 2312 | tf_op jit(solution)/shard_map/ppermute | solution.py:350
  74.2 3.6 %collective-permute-start.13 = (f32[3,64]{1,0:T(4,128)S(1)}, f32[3,64]{1,0:T(4,128)S(1)}, u32[]{:S(2)}, u32[]{:S(2)}) collective-permute-start(f32[3,64]{1,0:T(4,128)S(1)} %get-tuple-element.70), channel_id=1, source_target_pairs={{0,2},{1,3},{2,0},{3,1},{4,6},{5,7},{6,4},{7,5},{8,10},{9,11},{10,... | collective-permute-start | bytes 2312 | tf_op jit(solution)/shard_map/ppermute | solution.py:350
  74.7 3.1 %collective-permute-start.14 = (f32[3,64]{1,0:T(4,128)S(1)}, f32[3,64]{1,0:T(4,128)S(1)}, u32[]{:S(2)}, u32[]{:S(2)}) collective-permute-start(f32[3,64]{1,0:T(4,128)S(1)} %get-tuple-element.71), channel_id=1, source_target_pairs={{0,3},{1,2},{2,1},{3,0},{4,7},{5,6},{6,5},{7,4},{8,11},{9,10},{10,... | collective-permute-start | bytes 2312 | tf_op jit(solution)/shard_map/ppermute | solution.py:350
  85.2 3.9 %collective-permute-start.15 = (f32[3,512]{1,0:T(4,128)}, f32[3,512]{1,0:T(4,128)S(1)}, u32[]{:S(2)}, u32[]{:S(2)}) collective-permute-start(f32[3,512]{1,0:T(4,128)} %get-tuple-element.58), channel_id=1, source_target_pairs={{0,4},{4,0},{8,12},{12,8},{16,20},{20,16},{24,28},{28,24},{1,5},{5... | collective-permute-start | bytes 18440 | tf_op jit(solution)/shard_map/ppermute | solution.py:293
  85.8 6.6 %collective-permute-start.16 = (f32[3,512]{1,0:T(4,128)}, f32[3,512]{1,0:T(4,128)S(1)}, u32[]{:S(2)}, u32[]{:S(2)}) collective-permute-start(f32[3,512]{1,0:T(4,128)} %get-tuple-element.59), channel_id=1, source_target_pairs={{4,8},{8,4},{12,16},{16,12},{20,24},{24,20},{28,0},{0,28},{5,9},{9... | collective-permute-start | bytes 18440 | tf_op jit(solution)/shard_map/ppermute | solution.py:294
  87.3 5.1 %collective-permute-start.17 = (f32[3,512]{1,0:T(4,128)}, f32[3,512]{1,0:T(4,128)S(1)}, u32[]{:S(2)}, u32[]{:S(2)}) collective-permute-start(f32[3,512]{1,0:T(4,128)} %get-tuple-element.60), channel_id=1, source_target_pairs={{0,1},{1,0},{2,3},{3,2},{4,5},{5,4},{6,7},{7,6},{8,9},{9,8},{10,11... | collective-permute-start | bytes 18440 | tf_op jit(solution)/shard_map/ppermute | solution.py:295
  87.3 5.1 %collective-permute-start.18 = (f32[3,512]{1,0:T(4,128)}, f32[3,512]{1,0:T(4,128)S(1)}, u32[]{:S(2)}, u32[]{:S(2)}) collective-permute-start(f32[3,512]{1,0:T(4,128)} %get-tuple-element.61), channel_id=1, source_target_pairs={{1,2},{2,1},{3,0},{0,3},{5,6},{6,5},{7,4},{4,7},{9,10},{10,9},{11,... | collective-permute-start | bytes 18440 | tf_op jit(solution)/shard_map/ppermute | solution.py:296
  99.5 3.9 %collective-permute-start.19 = (f32[3,512]{1,0:T(4,128)}, f32[3,512]{1,0:T(4,128)S(1)}, u32[]{:S(2)}, u32[]{:S(2)}) collective-permute-start(f32[3,512]{1,0:T(4,128)} %get-tuple-element.64), channel_id=1, source_target_pairs={{0,4},{4,0},{8,12},{12,8},{16,20},{20,16},{24,28},{28,24},{1,5},{5... | collective-permute-start | bytes 18440 | tf_op jit(solution)/shard_map/ppermute | solution.py:293
  99.6 6.6 %collective-permute-start.20 = (f32[3,512]{1,0:T(4,128)}, f32[3,512]{1,0:T(4,128)S(1)}, u32[]{:S(2)}, u32[]{:S(2)}) collective-permute-start(f32[3,512]{1,0:T(4,128)} %get-tuple-element.65), channel_id=1, source_target_pairs={{4,8},{8,4},{12,16},{16,12},{20,24},{24,20},{28,0},{0,28},{5,9},{9... | collective-permute-start | bytes 18440 | tf_op jit(solution)/shard_map/ppermute | solution.py:294
  101.0 5.1 %collective-permute-start.21 = (f32[3,512]{1,0:T(4,128)}, f32[3,512]{1,0:T(4,128)S(1)}, u32[]{:S(2)}, u32[]{:S(2)}) collective-permute-start(f32[3,512]{1,0:T(4,128)} %get-tuple-element.66), channel_id=1, source_target_pairs={{0,1},{1,0},{2,3},{3,2},{4,5},{5,4},{6,7},{7,6},{8,9},{9,8},{10,11... | collective-permute-start | bytes 18440 | tf_op jit(solution)/shard_map/ppermute | solution.py:295
  101.3 4.9 %collective-permute-start.22 = (f32[3,512]{1,0:T(4,128)}, f32[3,512]{1,0:T(4,128)S(1)}, u32[]{:S(2)}, u32[]{:S(2)}) collective-permute-start(f32[3,512]{1,0:T(4,128)} %get-tuple-element.67), channel_id=1, source_target_pairs={{1,2},{2,1},{3,0},{0,3},{5,6},{6,5},{7,4},{4,7},{9,10},{10,9},{11,... | collective-permute-start | bytes 18440 | tf_op jit(solution)/shard_map/ppermute | solution.py:296
  (20 other events, 19.0 us)

commit v2 on v1

v2 whole, which is shorter than its diff:
```python
import jax
import jax.numpy as jnp
from jax import lax
from jax.experimental import pallas as pl
from jax.experimental.pallas import tpu as pltpu
from jax.sharding import PartitionSpec as P

POST = 2
DAMPING = 0.6
WINDOW = 64
LANES = 128
BIG = 16
CHUNKS = 9
F32 = jnp.float32
BF16 = jnp.bfloat16


def two_parts(value):
    high = value.astype(BF16)
    low = (value - high.astype(F32)).astype(BF16)
    return high, low


def nt_dot(left, right):
    return lax.dot_general(left, right, (((1,), (1,)), ((), ())), preferred_element_type=F32)


def low_onehot(index_row):
    low = index_row & (LANES - 1)
    rows = lax.broadcasted_iota(jnp.int32, (LANES, index_row.shape[1]), 0)
    return jnp.where(rows == low, 1.0, 0.0).astype(BF16)


def high_onehot(index_row, count):
    rows = lax.broadcasted_iota(jnp.int32, (count, index_row.shape[1]), 0)
    return jnp.where(rows == (index_row >> 7), 1.0, 0.0).astype(BF16)


def field_parts(field):
    high, low = two_parts(field)
    return jnp.concatenate([high, low], axis=1)


def gather_slot(parts, onehot, index_row):
    count = parts.shape[0] // 3
    picked = jnp.dot(parts, jnp.concatenate([onehot, onehot], axis=0), preferred_element_type=F32)
    rows = lax.broadcasted_iota(jnp.int32, (count, index_row.shape[1]), 0)
    mask = rows == (index_row >> 7)
    return [
        jnp.sum(jnp.where(mask, picked[c * count:(c + 1) * count], 0.0), axis=0, keepdims=True)
        for c in range(3)
    ]


def scatter_slot(rows, low_hot, high_hot):
    spread = []
    for row in rows:
        wide = jnp.broadcast_to(row, (16, row.shape[1])).astype(BF16)
        spread.append(jnp.concatenate([wide] * (high_hot.shape[0] // 16), axis=0) * high_hot)
    return nt_dot(jnp.concatenate(spread, axis=0), low_hot)


def join_parts(total):
    half = total.shape[0] // 2
    return total[:half] + total[half:]


def send_faces(field, first, index, low_hot, out_refs):
    parts = field_parts(field)
    for slot in range(4):
        rows = gather_slot(parts, low_hot[first + slot], index[first + slot:first + slot + 1, :])
        out_refs[slot][...] = jnp.concatenate(rows, axis=0)


def add_faces(first, low_hot, high_hot, in_refs):
    total = None
    for slot in range(4):
        value = in_refs[slot][...]
        high = value.astype(BF16).astype(F32)
        low = value - high
        rows = [part[c:c + 1] for part in (high, low) for c in range(3)]
        got = scatter_slot(rows, low_hot[first + slot], high_hot[first + slot])
        total = got if total is None else total + got
    return join_parts(total)


def scatter_elements(high_s, low_s, first, low_hot, high_hot):
    total = None
    for i in range(first):
        rows = [
            part[c * first + i:c * first + i + 1, :]
            for part in (high_s, low_s) for c in range(3)
        ]
        got = scatter_slot(rows, low_hot[i], high_hot[i])
        total = got if total is None else total + got
    return join_parts(total)


def store_parts(value, high_s, low_s):
    high = value.astype(BF16).astype(F32)
    high_s[...] = high
    low_s[...] = value - high


def element_apply(field, mesh_refs, scratch):
    index, coef, mat_high, mat_low, low_hot, high_hot = mesh_refs
    got_s, high_s, low_s = scratch
    first = low_hot.shape[0] - 4
    parts = field_parts(field)
    got_s[80:, :] = jnp.zeros_like(got_s[80:, :])
    for i in range(first):
        rows = gather_slot(parts, low_hot[i], index[i:i + 1, :])
        for c in range(3):
            got_s[c * first + i:c * first + i + 1, :] = rows[c]
    got_high, got_low = two_parts(got_s[...])
    product = (
        jnp.dot(mat_high[...], got_high, preferred_element_type=F32)
        + jnp.dot(mat_high[...], got_low, preferred_element_type=F32)
        + jnp.dot(mat_low[...], got_high, preferred_element_type=F32)
    )
    store_parts(product * coef[...], high_s, low_s)
    return scatter_elements(high_s, low_s, first, low_hot, high_hot)


def finish_apply(field, mass, mesh_refs, scratch, local_out, faces_out):
    local = mass[...] * field + element_apply(field, mesh_refs, scratch)
    local_out[...] = local
    index, low_hot = mesh_refs[0], mesh_refs[4]
    send_faces(local, low_hot.shape[0] - 4, index, low_hot, faces_out)


def diag_kernel(par, nodes_h, coef_h, mass_h, right_h, faces_h, matrix_h,
                diag_out, s0, s1, s2, s3, index, coef, mass, right, mat_high, mat_low, low_hot, high_hot,
                nodes_s, faces_s, matrix_s, pad_s, high_s, low_s, sems):
    moves = [(nodes_h, nodes_s), (coef_h, coef), (mass_h, mass), (right_h, right),
             (faces_h, faces_s), (matrix_h, matrix_s)]
    copies = [pltpu.make_async_copy(src, dst, sems.at[n]) for n, (src, dst) in enumerate(moves)]
    for copy in copies:
        copy.start()
    first = low_hot.shape[0] - 4
    count = high_hot.shape[1]
    size = matrix_h.shape[0]
    pad_s[...] = jnp.zeros_like(pad_s)
    copies[0].wait()
    for i in range(first):
        for t in range(nodes_s.shape[1]):
            index[i:i + 1, t * LANES:(t + 1) * LANES] = nodes_s[i, t:t + 1, :]
    copies[4].wait()
    for slot, face in enumerate([1 - par[0], par[0], 3 - par[1], 2 + par[1]]):
        index[first + slot:first + slot + 1, :] = faces_s[pl.ds(face, 1), :]
    copies[5].wait()
    pad_s[:size, :size] = matrix_s[...]
    mat_high[...], mat_low[...] = two_parts(pad_s[...])
    rows = lax.broadcasted_iota(jnp.int32, pad_s.shape, 0)
    cols = lax.broadcasted_iota(jnp.int32, pad_s.shape, 1)
    main = jnp.sum(jnp.where(rows == cols, pad_s[...], 0.0), axis=1, keepdims=True)
    copies[1].wait()
    store_parts(main * coef[...], high_s, low_s)
    total = None
    for i in range(first + 4):
        row = index[i:i + 1, :]
        low = low_onehot(row)
        high = high_onehot(row, count)
        low_hot[i] = low
        high_hot[i] = high
        if i < first:
            rows = [
                part[c * first + i:c * first + i + 1, :]
                for part in (high_s, low_s) for c in range(3)
            ]
            got = scatter_slot(rows, low, high)
            total = got if total is None else total + got
    copies[2].wait()
    diag = mass[...] + join_parts(total)
    diag_out[...] = diag
    send_faces(diag, first, index, low_hot, (s0, s1, s2, s3))
    copies[3].wait()


def first_kernel(diag, g0, g1, g2, g3, mass, right, index, coef, mat_high, mat_low, low_hot, high_hot,
                 gain_out, field_out, local_out, s0, s1, s2, s3, *scratch):
    total = diag[...] + add_faces(low_hot.shape[0] - 4, low_hot, high_hot, (g0, g1, g2, g3))
    gain = DAMPING / total
    gain_out[...] = gain
    field = gain * right[...]
    field_out[...] = field
    finish_apply(field, mass, (index, coef, mat_high, mat_low, low_hot, high_hot), scratch,
                 local_out, (s0, s1, s2, s3))


def sweep_kernel(local_in, g0, g1, g2, g3, field_in, gain, mass, right, index, coef, mat_high, mat_low,
                 low_hot, high_hot, field_out, local_out, s0, s1, s2, s3, *scratch):
    total = local_in[...] + add_faces(low_hot.shape[0] - 4, low_hot, high_hot, (g0, g1, g2, g3))
    field = field_in[...] + gain[...] * (right[...] - total)
    field_out[...] = field
    finish_apply(field, mass, (index, coef, mat_high, mat_low, low_hot, high_hot), scratch,
                 local_out, (s0, s1, s2, s3))


def with_move(kernel, n_in, n_out, first_row):
    def moving(*refs):
        source, ins = refs[0], refs[1:1 + n_in]
        outs, target = refs[1 + n_in:1 + n_in + n_out], refs[1 + n_in + n_out]
        scratch, sem = refs[2 + n_in + n_out:-1], refs[-1]
        size = target.shape[0] // CHUNKS

        def chunk(n):
            start = pl.multiple_of(n * size, 8)
            return pltpu.make_async_copy(
                source.at[pl.ds(first_row + start, size), :], target.at[pl.ds(start, size), :], sem.at[n])

        @pl.loop(0, CHUNKS)
        def _(n):
            chunk(n).start()

        kernel(*ins, *outs, *scratch)

        @pl.loop(0, CHUNKS)
        def _(n):
            chunk(n).wait()

    return moving


def last_kernel(local_in, g0, g1, g2, g3, field_in, gain, right, low_hot, high_hot, field_out):
    total = local_in[...] + add_faces(low_hot.shape[0] - 4, low_hot, high_hot, (g0, g1, g2, g3))
    field_out[...] = field_in[...] + gain[...] * (right[...] - total)


def prepare_kernel(width, par, coarse_h, weights_h, table, coarse, weights, sems):
    copies = [pltpu.make_async_copy(coarse_h, coarse, sems.at[0]),
              pltpu.make_async_copy(weights_h, weights, sems.at[1])]
    for copy in copies:
        copy.start()
    for copy in copies:
        copy.wait()
    total = None
    for q in range(coarse.shape[0]):
        offset = coarse[q:q + 1, :] - par[2]
        offset = jnp.where(offset < 0, offset + width, offset)
        rows = lax.broadcasted_iota(jnp.int32, (WINDOW, coarse.shape[1]), 0)
        part = jnp.where(rows == offset, weights[q:q + 1, :], 0.0)
        total = part if total is None else total + part
    high, low = two_parts(total)
    table[:WINDOW, :] = high
    table[WINDOW:, :] = low


def restrict_kernel(local_in, g0, g1, g2, g3, right, low_hot, high_hot, table, out, res_s, flat_s):
    count = high_hot.shape[1]
    total = local_in[...] + add_faces(low_hot.shape[0] - 4, low_hot, high_hot, (g0, g1, g2, g3))
    res_s[...] = right[...] - total
    flat_s[...] = jnp.zeros_like(flat_s)
    for h in range(count):
        for c in range(3):
            flat_s[c:c + 1, h * LANES:(h + 1) * LANES] = res_s[c * count + h:c * count + h + 1, :]
    high, low = two_parts(flat_s[...])
    wide = nt_dot(high, table[...])
    both = wide + pltpu.roll(wide, WINDOW, 1) + nt_dot(low, table[...])
    lanes = lax.broadcasted_iota(jnp.int32, both.shape, 1)
    window = jnp.where(lanes < WINDOW, both, 0.0)[:4]
    for other in range(out.shape[0]):
        out[other] = window


def prolong_kernel(w0, *refs):
    extra = refs[:-22]
    (field_in, table, mass, index, coef, mat_high, mat_low, low_hot, high_hot,
     field_out, local_out, s0, s1, s2, s3, got_s, high_s, low_s, flat_s, res_s, wide_s, low_w) = refs[-22:]
    count = high_hot.shape[1]
    window = w0[...]
    for ref in extra:
        window = window + ref[...]
    high = window.astype(BF16).astype(F32)
    low = window - high
    flat_s[...] = (
        jnp.dot((high + pltpu.roll(high, WINDOW, 1)).astype(BF16), table[...], preferred_element_type=F32)
        + jnp.dot(low.astype(BF16), table[...], preferred_element_type=F32)
    )
    for h in range(count):
        for c in range(3):
            res_s[c * count + h:c * count + h + 1, :] = flat_s[c:c + 1, h * LANES:(h + 1) * LANES]
    field = field_in[...] + res_s[...]
    field_out[...] = field
    finish_apply(field, mass, (index, coef, mat_high, mat_low, low_hot, high_hot), (got_s, high_s, low_s),
                 local_out, (s0, s1, s2, s3))


def coarse_kernel(n_dev, width, par, windows, upper, lower, *refs):
    outs, (rhs_s, half_s) = refs[:n_dev], refs[n_dev:]
    total = windows.shape[0]
    stride = width // total
    tiles = width // LANES
    lanes = lax.broadcasted_iota(jnp.int32, (4, LANES), 1)
    sums = [jnp.zeros((4, LANES), F32)] * tiles
    for other in range(total):
        tile, shift = divmod(other * stride, LANES)
        window = windows[other]
        if shift:
            window = pltpu.roll(window, shift, 1)
        if shift + WINDOW > LANES:
            sums[tile] = sums[tile] + jnp.where(lanes >= shift, window, 0.0)
            after = (tile + 1) % tiles
            sums[after] = sums[after] + jnp.where(lanes < shift, window, 0.0)
        else:
            sums[tile] = sums[tile] + window
    for tile in range(tiles):
        for c in range(3):
            rhs_s[c * tiles + tile] = jnp.broadcast_to(sums[tile][c:c + 1], (8, LANES))
    rows = upper.shape[0]
    block = 64

    def first_product(factor, offset):
        def body(step, carry):
            start = pl.multiple_of(step * block, block)
            acc = [None] * (block // 8)
            for tile in range(3 * tiles):
                value = rhs_s[tile]
                piece = factor[pl.ds(start, block), tile * LANES:(tile + 1) * LANES]
                for r in range(block // 8):
                    term = piece[r * 8:(r + 1) * 8] * value
                    acc[r] = term if acc[r] is None else acc[r] + term
            half_s[pl.ds(offset + start, block), :] = jnp.concatenate(acc, axis=0)
            return carry

        lax.fori_loop(0, rows // block, body, 0)

    first_product(upper, 0)
    first_product(lower, rows)
    half_s[...] = jnp.broadcast_to(jnp.sum(half_s[...], axis=1, keepdims=True), half_s.shape)

    base = par[3] * stride
    first_tile = base // LANES
    rest = base - first_tile * LANES
    span = -(-(LANES - 1 + (n_dev - 1) * stride + WINDOW) // LANES)
    starts = []
    for c in range(3):
        for t in range(span):
            tile = first_tile + t
            tile = jnp.where(tile >= tiles, tile - tiles, tile)
            starts.append(pl.multiple_of((c * tiles + tile) * LANES, LANES))

    def second_product(factor, offset, sums):
        def body(step, acc):
            start = pl.multiple_of(step * block, block)
            half = half_s[pl.ds(offset + start, block), :]
            out = []
            for n, lane in enumerate(starts):
                piece = factor[pl.ds(start, block), pl.ds(lane, LANES)] * half
                value = acc[n]
                for r in range(block // 8):
                    value = value + piece[r * 8:(r + 1) * 8]
                out.append(value)
            return tuple(out)

        return lax.fori_loop(0, rows // block, body, sums)

    acc = tuple(jnp.zeros((8, LANES), F32) for _ in starts)
    acc = second_product(lower, rows, second_product(upper, 0, acc))
    parts = [jnp.sum(value, axis=0, keepdims=True) for value in acc]
    comps = [jnp.concatenate(parts[c * span:(c + 1) * span], axis=1) for c in range(3)]
    table = jnp.concatenate(comps + [jnp.zeros((5, span * LANES), F32)], axis=0)
    lanes = lax.broadcasted_iota(jnp.int32, (8, LANES), 1)
    for step in range(n_dev):
        shift = rest + (par[4] ^ step) * stride
        moved = pltpu.roll(table, span * LANES - shift, 1)[:, :LANES]
        outs[step][...] = jnp.where(lanes < WINDOW, moved, 0.0)


def local_program(mesh_shape, right_side, elem_nodes, elem_coef, node_mass, face_slots, coarse_nodes,
                  coarse_weights, elem_matrix, chol_inverse):
    n_grp, n_dev = mesh_shape
    total = n_grp * n_dev
    nodes_count = right_side.shape[-1]
    hi = nodes_count // LANES
    local_nodes, elements = elem_nodes.shape[2:]
    slots = face_slots.shape[-1]
    width = chol_inverse.shape[1] // 3
    grp = lax.axis_index("grp")
    dev = lax.axis_index("dev")
    home = (grp * n_dev + dev) * width // total
    par = jnp.stack([grp & 1, dev & 1, home, grp * n_dev, dev]).astype(jnp.int32)

    right = right_side.reshape(3 * hi, LANES)
    mass = node_mass.reshape(3 * hi, LANES)
    nodes = elem_nodes.reshape(local_nodes, elements // LANES, LANES)
    coef = elem_coef[0]
    faces = face_slots[0, 0]
    coarse = coarse_nodes[0, 0]
    weights = coarse_weights[0, 0]

    smem = pl.BlockSpec(memory_space=pltpu.SMEM)
    vmem = pl.BlockSpec(memory_space=pltpu.VMEM)
    hbm = pl.BlockSpec(memory_space=pltpu.HBM)

    def shape(*dims, dtype=F32):
        return jax.ShapeDtypeStruct(dims, dtype)

    def call(kernel, outs, scratch, specs, *args, limit=8):
        args = [
            pltpu.with_memory_space_constraint(arg, pltpu.HBM) if n < len(specs) and specs[n] is hbm else arg
            for n, arg in enumerate(args)
        ]
        return pl.pallas_call(
            kernel,
            out_shape=outs,
            in_specs=specs + [vmem] * (len(args) - len(specs)),
            out_specs=jax.tree.map(lambda _: vmem, outs),
            scratch_shapes=scratch,
            compiler_params=pltpu.CompilerParams(vmem_limit_bytes=limit << 20),
        )(*args)

    field_t = shape(3 * hi, LANES)
    face_t = [shape(3, slots)] * 4
    rows = 3 * local_nodes
    padded = -(-rows // LANES) * LANES
    part_rows = -(-rows // 16) * 16
    lists = local_nodes + 4
    parts_s = [pltpu.VMEM((part_rows, elements), F32)] * 2
    apply_s = [pltpu.VMEM((padded, elements), F32)] + parts_s
    flat_s = pltpu.VMEM((8, nodes_count), F32)
    field_s = pltpu.VMEM((3 * hi, LANES), F32)

    def pairs(axis, parity):
        count = n_grp if axis == 0 else n_dev
        out = []
        for g in range(n_grp):
            for d in range(n_dev):
                here = (g, d)[axis]
                there = here + 1 if here % 2 == parity else here - 1
                if axis == 0:
                    other = (there, d) if 0 <= there < count else (g, d ^ 1)
                else:
                    other = (g, there % count)
                out.append((g * n_dev + d, other[0] * n_dev + other[1]))
        return out

    routes = [pairs(axis, parity) for axis in (0, 1) for parity in (0, 1)]

    def swap(faces_out):
        return [lax.ppermute(face, ("grp", "dev"), route) for face, route in zip(faces_out, routes)]

    diag, *out = call(
        diag_kernel,
        [field_t] + face_t + [
            shape(-(-lists // 8) * 8, elements, dtype=jnp.int32), shape(1, elements), field_t, field_t,
            shape(part_rows, padded, dtype=BF16), shape(part_rows, padded, dtype=BF16),
            shape(lists, LANES, elements, dtype=BF16), shape(lists, hi, elements, dtype=BF16)],
        [pltpu.VMEM(nodes.shape, jnp.int32), pltpu.VMEM(faces.shape, jnp.int32),
         pltpu.VMEM(elem_matrix.shape, F32), pltpu.VMEM((part_rows, padded), F32)] + parts_s
        + [pltpu.SemaphoreType.DMA((6,))],
        [smem] + [hbm] * 6, par, nodes, coef, mass, right, faces, elem_matrix)
    out, (index, coef, mass, right, mat_high, mat_low, low_hot, high_hot) = out[:4], out[4:]
    element = (index, coef, mat_high, mat_low, low_hot, high_hot)

    got = swap(out)

    def prepare(*refs):
        prepare_kernel(width, *refs)

    table = call(
        prepare, shape(2 * WINDOW, nodes_count, dtype=BF16),
        [pltpu.VMEM(coarse.shape, jnp.int32), pltpu.VMEM(weights.shape, F32), pltpu.SemaphoreType.DMA((2,))],
        [smem, hbm, hbm], par, coarse, weights)
    half_rows = chol_inverse.shape[0] // 2
    half_t = [pltpu.VMEM((half_rows, 3 * width), F32)]

    def call_moving(kernel, outs, first_row, *args):
        return call(
            with_move(kernel, len(args), len(outs), first_row), outs + half_t,
            apply_s + [pltpu.SemaphoreType.DMA((CHUNKS,))], [hbm], chol_inverse, *args, limit=BIG)

    gain, field, local, *out, upper = call_moving(
        first_kernel, [field_t] * 3 + face_t, 0, diag, *got, mass, right, *element)
    got = swap(out)
    field, local, *out, lower = call_moving(
        sweep_kernel, [field_t] * 2 + face_t, half_rows, local, *got, field, gain, mass, right, *element)
    got = swap(out)
    window = call(
        restrict_kernel, shape(total, 4, LANES), [field_s, flat_s], [],
        local, *got, right, low_hot, high_hot, table)
    windows = lax.all_to_all(window, ("grp", "dev"), 0, 0)

    def coarse_solve(*refs):
        coarse_kernel(n_dev, width, *refs)

    parts = call(
        coarse_solve, [shape(8, LANES)] * n_dev,
        [pltpu.VMEM((3 * width // LANES, 8, LANES), F32), pltpu.VMEM((chol_inverse.shape[0], LANES), F32)],
        [smem], par, windows, upper, lower)
    corrections = [parts[0]]
    for step in range(1, n_dev):
        corrections.append(lax.ppermute(parts[step], "dev", [(i, i ^ step) for i in range(n_dev)]))

    field, local, *out = call(
        prolong_kernel, [field_t] * 2 + face_t, apply_s + [flat_s, field_s, field_s, field_s], [],
        *corrections, field, table, mass, *element)
    for _ in range(POST - 1):
        got = swap(out)
        field, local, *out = call(
            sweep_kernel, [field_t] * 2 + face_t, apply_s, [], local, *got, field, gain, mass, right, *element)
    got = swap(out)
    field = call(last_kernel, field_t, [], [], local, *got, field, gain, right, low_hot, high_hot)
    return field.reshape(1, 1, 3, nodes_count)


def solution(mesh):
    mesh_shape = (mesh.shape["grp"], mesh.shape["dev"])

    def local(*args):
        return local_program(mesh_shape, *args)

    return jax.shard_map(
        local,
        mesh=mesh,
        in_specs=(
            P("grp", "dev", None, None),
            P("grp", "dev", None, None),
            P("grp", "dev", None),
            P("grp", "dev", None, None),
            P("grp", "dev", None, None),
            P("grp", "dev", None, None),
            P("grp", "dev", None, None),
            P(),
            P("dev", None),
        ),
        out_specs=P("grp", "dev", None, None),
        check_vma=False,
    )
```

time: 109 us -> 72.4 us (0.66)
  Pallas kernels: 48.6 us -> 28.3 us
  blocking collectives: 0 us -> 12.3 us
  waiting for transfers between devices: 19.6 us -> 9.74 us
  starting transfers between devices: 30.3 us -> 21.6 us
  local copies, waits for them, and re-layouts: 7.83 us -> 0.08 us
  other arithmetic: 2.29 us -> 0 us
    pallas_call x9, Pallas kernels: 48.6 us -> 28.3 us  [call(): pl.pallas_call(kernel, out_shape=outs, in_specs=specs + [vmem] * (len(arg...]
    all_to_all x0 -> x1, blocking collectives: none -> 12.3 us  [local_program(): windows = lax.all_to_all(window, ('grp', 'dev'), 0, 0)]
    all_to_all x1 -> x0, waiting for transfers between devices: 7.23 us -> none  [local_program(): windows = lax.all_to_all(sent, ('grp', 'dev'), 0, 0)]
    unnamed x43 -> x0, local copies, waits for them, and re-layouts: 5.18 us -> none
    ppermute x23, starting transfers between devices: 26.7 us -> 21.6 us  [the longest x20 19.7 us: swap(): lax.ppermute(face, ('grp', 'dev'), route)]
    all_to_all x1 -> x0, starting transfers between devices: 3.58 us -> none  [local_program(): windows = lax.all_to_all(sent, ('grp', 'dev'), 0, 0)]
    ppermute x23, waiting for transfers between devices: 12.3 us -> 9.74 us  [the longest x20 7.88 us: swap(): lax.ppermute(face, ('grp', 'dev'), route)]
  transfers between devices with their start and end apart: 24 -> 23, of which waited for: 9 -> 7; matrix products, arithmetic and copies ran while one was open for 0% -> 0% of each run, Pallas kernels for 2% -> 3%
where the time goes in v2:
time: 72.4 us; the launch traced here: 72.2 us
  Pallas kernels  28.3 us (39%)
  starting transfers between devices  21.6 us (30%)
  blocking collectives  12.3 us (17%)
  waiting for transfers between devices  9.74 us (13%)
    pallas_call x9, Pallas kernels, call(): pl.pallas_call(kernel, out_shape=outs, in_specs=specs + [vmem] * (len(arg...  28.3 us
    ppermute x20, starting transfers between devices, swap(): lax.ppermute(face, ('grp', 'dev'), route)  19.7 us
    all_to_all x1, blocking collectives, local_program(): windows = lax.all_to_all(window, ('grp', 'dev'), 0, 0)  12.3 us
    ppermute x20, waiting for transfers between devices, swap(): lax.ppermute(face, ('grp', 'dev'), route)  7.88 us
    ppermute x3, starting transfers between devices, local_program(): lax.ppermute(parts[step], 'dev', [(i, i ^ step) for i in range(n_dev)])  1.93 us
    ppermute x3, waiting for transfers between devices, local_program(): lax.ppermute(parts[step], 'dev', [(i, i ^ step) for i in range(n_dev)])  1.86 us
  transfers between devices with their start and end apart: 23, of which 7 were waited for; matrix products, arithmetic and copies ran while one was open for 0% of the time, Pallas kernels for 3%

profile of v2, /device:TPU:0, one launch (start us, length us, event | category | flops | bytes accessed | tf_op | source)
XLA Modules:
  0.0 72.2 jit_solution(2650459295280837144)
XLA Ops:
  0.1 4.4 %shard_map.91 = (f32[96,128]{1,0:T(8,128)S(1)}, f32[3,512]{1,0:T(4,128)S(1)}, f32[3,512]{1,0:T(4,128)S(1)}, f32[3,512]{1,0:T(4,128)S(1)}, f32[3,512]{1,0:T(4,128...) custom-call(s32[5]{0:T(128)S(1)} %stack.23.par.refs_0_, ...), custom_call_target="tpu_custom_call" | custom-call | tf_op jit(solution)/shard_map/pallas_call | solution.py:404
  4.4 3.1 %collective-permute-start = (f32[3,512]{1,0:T(4,128)S(1)}, f32[3,512]{1,0:T(4,128)S(1)}, u32[]{:S(2)}, u32[]{:S(2)}) collective-permute-start(f32[3,512]{1,0:T(4,128)S(1)} %get-tuple-element.50), channel_id=1, source_target_pairs={{0,4},{1,5},{2,6},{3,7},{4,0},{5,1},{6,2},{7,3},{8,12},{9,13},{10,... | collective-permute-start | bytes 18440 | tf_op jit(solution)/shard_map/ppermute | solution.py:441
  8.0 1.1 %collective-permute-start.3 = (f32[3,512]{1,0:T(4,128)S(1)}, f32[3,512]{1,0:T(4,128)S(1)}, u32[]{:S(2)}, u32[]{:S(2)}) collective-permute-start(f32[3,512]{1,0:T(4,128)S(1)} %get-tuple-element.53), channel_id=1, source_target_pairs={{0,3},{1,2},{2,1},{3,0},{4,7},{5,6},{6,5},{7,4},{8,11},{9,10},{10,... | collective-permute-start | bytes 18440 | tf_op jit(solution)/shard_map/ppermute | solution.py:441
  9.1 1.9 %collective-permute-done.3.refs_5_ = f32[3,512]{1,0:T(4,128)S(1)} collective-permute-done((f32[3,512]{1,0:T(4,128)S(1)}, f32[3,512]{1,0:T(4,128)S(1)}, u32[]{:S(2)}, u32[]{:S(2)}) %collective-permute-start.3) | collective-permute-done | bytes 6176 | tf_op jit(solution)/shard_map/ppermute | solution.py:441
  11.1 4.1 %shard_map.92 = (f32[96,128]{1,0:T(8,128)S(1)}, f32[96,128]{1,0:T(8,128)S(1)}, f32[96,128]{1,0:T(8,128)S(1)}, f32[3,512]{1,0:T(4,128)S(1)}, f32[3,512]{1,0:T(4,1...) custom-call(f32[1152,4608]{1,0:T(8,128)} %refs_0_.3, ...), custom_call_target="tpu_custom_call" | custom-call | tf_op jit(solution)/shard_map/pallas_call | solution.py:404
  15.2 2.6 %collective-permute-start.4 = (f32[3,512]{1,0:T(4,128)S(1)}, f32[3,512]{1,0:T(4,128)S(1)}, u32[]{:S(2)}, u32[]{:S(2)}) collective-permute-start(f32[3,512]{1,0:T(4,128)S(1)} %get-tuple-element.63), channel_id=1, source_target_pairs={{0,4},{1,5},{2,6},{3,7},{4,0},{5,1},{6,2},{7,3},{8,12},{9,13},{10,... | collective-permute-start | bytes 18440 | tf_op jit(solution)/shard_map/ppermute | solution.py:441
  18.3 1.3 %collective-permute-start.7 = (f32[3,512]{1,0:T(4,128)S(1)}, f32[3,512]{1,0:T(4,128)S(1)}, u32[]{:S(2)}, u32[]{:S(2)}) collective-permute-start(f32[3,512]{1,0:T(4,128)S(1)} %get-tuple-element.66), channel_id=1, source_target_pairs={{0,3},{1,2},{2,1},{3,0},{4,7},{5,6},{6,5},{7,4},{8,11},{9,10},{10,... | collective-permute-start | bytes 18440 | tf_op jit(solution)/shard_map/ppermute | solution.py:441
  19.7 1.7 %collective-permute-done.7.refs_5_ = f32[3,512]{1,0:T(4,128)S(1)} collective-permute-done((f32[3,512]{1,0:T(4,128)S(1)}, f32[3,512]{1,0:T(4,128)S(1)}, u32[]{:S(2)}, u32[]{:S(2)}) %collective-permute-start.7) | collective-permute-done | bytes 6176 | tf_op jit(solution)/shard_map/ppermute | solution.py:441
  21.4 4.1 %shard_map.93 = (f32[96,128]{1,0:T(8,128)S(1)}, f32[96,128]{1,0:T(8,128)S(1)}, f32[3,512]{1,0:T(4,128)S(1)}, f32[3,512]{1,0:T(4,128)S(1)}, f32[3,512]{1,0:T(4,12...) custom-call(f32[1152,4608]{1,0:T(8,128)} %refs_0_.3, f32[96,128]{1,0:T(8,128)S(1)} %get-tuple-element.62.refs_1_, ...), custom_call_target="tpu_custom_call" | custom-call | tf_op jit(solution)/shard_map/pallas_call | solution.py:404
  25.8 1.4 %collective-permute-start.11 = (f32[3,512]{1,0:T(4,128)S(1)}, f32[3,512]{1,0:T(4,128)S(1)}, u32[]{:S(2)}, u32[]{:S(2)}) collective-permute-start(f32[3,512]{1,0:T(4,128)S(1)} %get-tuple-element.73), channel_id=1, source_target_pairs={{0,3},{1,2},{2,1},{3,0},{4,7},{5,6},{6,5},{7,4},{8,11},{9,10},{10,... | collective-permute-start | bytes 18440 | tf_op jit(solution)/shard_map/ppermute | solution.py:441
  27.2 2.6 %collective-permute-start.8 = (f32[3,512]{1,0:T(4,128)S(1)}, f32[3,512]{1,0:T(4,128)S(1)}, u32[]{:S(2)}, u32[]{:S(2)}) collective-permute-start(f32[3,512]{1,0:T(4,128)S(1)} %get-tuple-element.70), channel_id=1, source_target_pairs={{0,4},{1,5},{2,6},{3,7},{4,0},{5,1},{6,2},{7,3},{8,12},{9,13},{10,... | collective-permute-start | bytes 18440 | tf_op jit(solution)/shard_map/ppermute | solution.py:441
  30.0 2.0 %shard_map.94.table.refs_4_ = bf16[128,4096]{1,0:T(8,128)(2,1)S(1)} custom-call(s32[5]{0:T(128)S(1)} %stack.23.par.refs_0_, s32[4,4096]{1,0:T(4,128)} %bitcast.13, f32[4,4096]{1,0:T(4,128)} %bitcast.14), custom_call_target="tpu_custom_call" | custom-call | tf_op jit(solution)/shard_map/pallas_call | solution.py:404
  32.1 1.1 %shard_map.95 = f32[32,4,128]{2,1,0:T(4,128)S(1)} custom-call(f32[96,128]{1,0:T(8,128)S(1)} %get-tuple-element.69.local_in, f32[3,512]{1,0:T(4,128)S(1)} %collective-permute-done.8.g0, f32[3,512]{1,0:T(4,128)S(1)} %collective-permute-done.9.g1, f32[3,512]{1,0:T(4,128)S(1)} %collective-permute-done.10.g2, f32[3,512]{1,0:T(4,128)S(1)} %collective-permute-done.11.g3, ...), custom_call_target="tpu_custom_call" | custom-call | tf_op jit(solution)/shard_map/pallas_call | solution.py:404
  33.2 12.3 %all_to_all.5.refs_1_ = f32[32,4,128]{2,1,0:T(4,128)S(1)} all-to-all(f32[32,4,128]{2,1,0:T(4,128)S(1)} %shard_map.95), channel_id=1, replica_groups=mesh['grp'=8,'dev'=4] {'grp','dev'}, dimensions={0} | all-to-all | bytes 131072 | tf_op jit(solution)/shard_map/all_to_all | solution.py:482
  45.5 4.0 %shard_map.96 = (f32[8,128]{1,0:T(8,128)S(1)}, f32[8,128]{1,0:T(8,128)S(1)}, f32[8,128]{1,0:T(8,128)S(1)}, f32[8,128]{1,0:T(8,128)S(1)}) custom-call(s32[5]{0:T(128)S(1)} %stack.23.par.refs_0_, f32[32,4,128]{2,1,0:T(4,128)S(1)} %all_to_all.5.refs_1_, f32[576,4608]{1,0:T(8,128)S(1)} %get-tuple-element.74.refs_2_, f32[576,4608]{1,0:T(8,128)S(1)} %get-tuple-element.75.refs_3_), custom_call_target="tpu_custom_call" | custom-call | tf_op jit(solution)/shard_map/pallas_call | solution.py:404
  50.2 1.3 %collective-permute-start.14 = (f32[8,128]{1,0:T(8,128)S(1)}, f32[8,128]{1,0:T(8,128)S(1)}, u32[]{:S(2)}, u32[]{:S(2)}) collective-permute-start(f32[8,128]{1,0:T(8,128)S(1)} %get-tuple-element.79), channel_id=1, source_target_pairs={{0,3},{1,2},{2,1},{3,0},{4,7},{5,6},{6,5},{7,4},{8,11},{9,10},{10,... | collective-permute-start | bytes 12296 | tf_op jit(solution)/shard_map/ppermute | solution.py:493
  51.5 1.9 %collective-permute-done.13.refs_1_ = f32[8,128]{1,0:T(8,128)S(1)} collective-permute-done((f32[8,128]{1,0:T(8,128)S(1)}, f32[8,128]{1,0:T(8,128)S(1)}, u32[]{:S(2)}, u32[]{:S(2)}) %collective-permute-start.13) | collective-permute-done | bytes 4128 | tf_op jit(solution)/shard_map/ppermute | solution.py:493
  53.3 3.8 %shard_map.97 = (f32[96,128]{1,0:T(8,128)S(1)}, f32[96,128]{1,0:T(8,128)S(1)}, f32[3,512]{1,0:T(4,128)S(1)}, f32[3,512]{1,0:T(4,128)S(1)}, f32[3,512]{1,0:T(4,128)S(1)}, /*index=5*/f32[3,512]{1,0:T(4,128)S(1)}) custom-call(f32[8,128]{1,0:T(8,128)S(1)} %get-tuple-element.76.w0, f32[8,128]{1,0:T(8,128)S(1)} %collective-permute-done.12.refs_0_, ...), custom_call_target="tpu_custom_call" | custom-call | tf_op jit(solution)/shard_map/pallas_call | solution.py:404
  59.3 1.5 %collective-permute-done.15.g0 = f32[3,512]{1,0:T(4,128)S(1)} collective-permute-done((f32[3,512]{1,0:T(4,128)S(1)}, f32[3,512]{1,0:T(4,128)S(1)}, u32[]{:S(2)}, u32[]{:S(2)}) %collective-permute-start.15) | collective-permute-done | bytes 6176 | tf_op jit(solution)/shard_map/ppermute | solution.py:441
  61.4 3.8 %shard_map.98 = (f32[96,128]{1,0:T(8,128)S(1)}, f32[96,128]{1,0:T(8,128)S(1)}, f32[3,512]{1,0:T(4,128)S(1)}, f32[3,512]{1,0:T(4,128)S(1)}, f32[3,512]{1,0:T(4,128)S(1)}, /*index=5*/f32[3,512]{1,0:T(4,128)S(1)}) custom-call(f32[96,128]{1,0:T(8,128)S(1)} %get-tuple-element.81.local_in, f32[3,512]{1,0:T(4,128)S(1)} %collective-permute-done.15.g0, ...), custom_call_target="tpu_custom_call" | custom-call | tf_op jit(solution)/shard_map/pallas_call | solution.py:404
  65.2 2.4 %collective-permute-start.19 = (f32[3,512]{1,0:T(4,128)S(1)}, f32[3,512]{1,0:T(4,128)S(1)}, u32[]{:S(2)}, u32[]{:S(2)}) collective-permute-start(f32[3,512]{1,0:T(4,128)S(1)} %get-tuple-element.88), channel_id=1, source_target_pairs={{0,4},{1,5},{2,6},{3,7},{4,0},{5,1},{6,2},{7,3},{8,12},{9,13},{10,... | collective-permute-start | bytes 18440 | tf_op jit(solution)/shard_map/ppermute | solution.py:441
  68.1 1.1 %collective-permute-start.22 = (f32[3,512]{1,0:T(4,128)S(1)}, f32[3,512]{1,0:T(4,128)S(1)}, u32[]{:S(2)}, u32[]{:S(2)}) collective-permute-start(f32[3,512]{1,0:T(4,128)S(1)} %get-tuple-element.91), channel_id=1, source_target_pairs={{0,3},{1,2},{2,1},{3,0},{4,7},{5,6},{6,5},{7,4},{8,11},{9,10},{10,... | collective-permute-start | bytes 18440 | tf_op jit(solution)/shard_map/ppermute | solution.py:441
  69.2 1.9 %collective-permute-done.22.g3 = f32[3,512]{1,0:T(4,128)S(1)} collective-permute-done((f32[3,512]{1,0:T(4,128)S(1)}, f32[3,512]{1,0:T(4,128)S(1)}, u32[]{:S(2)}, u32[]{:S(2)}) %collective-permute-start.22) | collective-permute-done | bytes 6176 | tf_op jit(solution)/shard_map/ppermute | solution.py:441
  71.2 1.0 %shard_map.99 = f32[96,128]{1,0:T(8,128)} custom-call(f32[96,128]{1,0:T(8,128)S(1)} %get-tuple-element.87.local_in, f32[3,512]{1,0:T(4,128)S(1)} %collective-permute-done.19.g0, f32[3,512]{1,0:T(4,128)S(1)} %collective-permute-done.20.g1, f32[3,512]{1,0:T(4,128)S(1)} %collective-permute-done.21.g2, f32[3,512]{1,0:T(4,128)S(1)} %collective-permute-done.22.g3, ...), custom_call_target="tpu_custom_call" | custom-call | tf_op jit(solution)/shard_map/pallas_call | solution.py:404
  (33 shorter events, 5.6 us)
Async XLA Ops:
  4.4 4.7 %collective-permute-start = (f32[3,512]{1,0:T(4,128)S(1)}, f32[3,512]{1,0:T(4,128)S(1)}, u32[]{:S(2)}, u32[]{:S(2)}) collective-permute-start(f32[3,512]{1,0:T(4,128)S(1)} %get-tuple-element.50), channel_id=1, source_target_pairs={{0,4},{1,5},{2,6},{3,7},{4,0},{5,1},{6,2},{7,3},{8,12},{9,13},{10,... | collective-permute-start | bytes 18440 | tf_op jit(solution)/shard_map/ppermute | solution.py:441
  7.5 1.6 %collective-permute-start.1 = (f32[3,512]{1,0:T(4,128)S(1)}, f32[3,512]{1,0:T(4,128)S(1)}, u32[]{:S(2)}, u32[]{:S(2)}) collective-permute-start(f32[3,512]{1,0:T(4,128)S(1)} %get-tuple-element.51), channel_id=1, source_target_pairs={{0,1},{1,0},{2,3},{3,2},{4,8},{5,9},{6,10},{7,11},{8,4},{9,5},{10,... | collective-permute-start | bytes 18440 | tf_op jit(solution)/shard_map/ppermute | solution.py:441
  7.5 1.6 %collective-permute-start.2 = (f32[3,512]{1,0:T(4,128)S(1)}, f32[3,512]{1,0:T(4,128)S(1)}, u32[]{:S(2)}, u32[]{:S(2)}) collective-permute-start(f32[3,512]{1,0:T(4,128)S(1)} %get-tuple-element.52), channel_id=1, source_target_pairs={{0,1},{1,0},{2,3},{3,2},{4,5},{5,4},{6,7},{7,6},{8,9},{9,8},{10,11... | collective-permute-start | bytes 18440 | tf_op jit(solution)/shard_map/ppermute | solution.py:441
  8.0 3.1 %collective-permute-start.3 = (f32[3,512]{1,0:T(4,128)S(1)}, f32[3,512]{1,0:T(4,128)S(1)}, u32[]{:S(2)}, u32[]{:S(2)}) collective-permute-start(f32[3,512]{1,0:T(4,128)S(1)} %get-tuple-element.53), channel_id=1, source_target_pairs={{0,3},{1,2},{2,1},{3,0},{4,7},{5,6},{6,5},{7,4},{8,11},{9,10},{10,... | collective-permute-start | bytes 18440 | tf_op jit(solution)/shard_map/ppermute | solution.py:441
  15.2 4.4 %collective-permute-start.4 = (f32[3,512]{1,0:T(4,128)S(1)}, f32[3,512]{1,0:T(4,128)S(1)}, u32[]{:S(2)}, u32[]{:S(2)}) collective-permute-start(f32[3,512]{1,0:T(4,128)S(1)} %get-tuple-element.63), channel_id=1, source_target_pairs={{0,4},{1,5},{2,6},{3,7},{4,0},{5,1},{6,2},{7,3},{8,12},{9,13},{10,... | collective-permute-start | bytes 18440 | tf_op jit(solution)/shard_map/ppermute | solution.py:441
  17.8 1.8 %collective-permute-start.5 = (f32[3,512]{1,0:T(4,128)S(1)}, f32[3,512]{1,0:T(4,128)S(1)}, u32[]{:S(2)}, u32[]{:S(2)}) collective-permute-start(f32[3,512]{1,0:T(4,128)S(1)} %get-tuple-element.64), channel_id=1, source_target_pairs={{0,1},{1,0},{2,3},{3,2},{4,8},{5,9},{6,10},{7,11},{8,4},{9,5},{10,... | collective-permute-start | bytes 18440 | tf_op jit(solution)/shard_map/ppermute | solution.py:441
  18.1 1.6 %collective-permute-start.6 = (f32[3,512]{1,0:T(4,128)S(1)}, f32[3,512]{1,0:T(4,128)S(1)}, u32[]{:S(2)}, u32[]{:S(2)}) collective-permute-start(f32[3,512]{1,0:T(4,128)S(1)} %get-tuple-element.65), channel_id=1, source_target_pairs={{0,1},{1,0},{2,3},{3,2},{4,5},{5,4},{6,7},{7,6},{8,9},{9,8},{10,11... | collective-permute-start | bytes 18440 | tf_op jit(solution)/shard_map/ppermute | solution.py:441
  18.3 3.1 %collective-permute-start.7 = (f32[3,512]{1,0:T(4,128)S(1)}, f32[3,512]{1,0:T(4,128)S(1)}, u32[]{:S(2)}, u32[]{:S(2)}) collective-permute-start(f32[3,512]{1,0:T(4,128)S(1)} %get-tuple-element.66), channel_id=1, source_target_pairs={{0,3},{1,2},{2,1},{3,0},{4,7},{5,6},{6,5},{7,4},{8,11},{9,10},{10,... | collective-permute-start | bytes 18440 | tf_op jit(solution)/shard_map/ppermute | solution.py:441
  25.5 6.5 %collective-permute-start.10 = (f32[3,512]{1,0:T(4,128)S(1)}, f32[3,512]{1,0:T(4,128)S(1)}, u32[]{:S(2)}, u32[]{:S(2)}) collective-permute-start(f32[3,512]{1,0:T(4,128)S(1)} %get-tuple-element.72), channel_id=1, source_target_pairs={{0,1},{1,0},{2,3},{3,2},{4,5},{5,4},{6,7},{7,6},{8,9},{9,8},{10,11... | collective-permute-start | bytes 18440 | tf_op jit(solution)/shard_map/ppermute | solution.py:441
  25.8 6.2 %collective-permute-start.11 = (f32[3,512]{1,0:T(4,128)S(1)}, f32[3,512]{1,0:T(4,128)S(1)}, u32[]{:S(2)}, u32[]{:S(2)}) collective-permute-start(f32[3,512]{1,0:T(4,128)S(1)} %get-tuple-element.73), channel_id=1, source_target_pairs={{0,3},{1,2},{2,1},{3,0},{4,7},{5,6},{6,5},{7,4},{8,11},{9,10},{10,... | collective-permute-start | bytes 18440 | tf_op jit(solution)/shard_map/ppermute | solution.py:441
  27.2 4.8 %collective-permute-start.8 = (f32[3,512]{1,0:T(4,128)S(1)}, f32[3,512]{1,0:T(4,128)S(1)}, u32[]{:S(2)}, u32[]{:S(2)}) collective-permute-start(f32[3,512]{1,0:T(4,128)S(1)} %get-tuple-element.70), channel_id=1, source_target_pairs={{0,4},{1,5},{2,6},{3,7},{4,0},{5,1},{6,2},{7,3},{8,12},{9,13},{10,... | collective-permute-start | bytes 18440 | tf_op jit(solution)/shard_map/ppermute | solution.py:441
  29.8 2.2 %collective-permute-start.9 = (f32[3,512]{1,0:T(4,128)S(1)}, f32[3,512]{1,0:T(4,128)S(1)}, u32[]{:S(2)}, u32[]{:S(2)}) collective-permute-start(f32[3,512]{1,0:T(4,128)S(1)} %get-tuple-element.71), channel_id=1, source_target_pairs={{0,1},{1,0},{2,3},{3,2},{4,8},{5,9},{6,10},{7,11},{8,4},{9,5},{10,... | collective-permute-start | bytes 18440 | tf_op jit(solution)/shard_map/ppermute | solution.py:441
  49.5 1.9 %collective-permute-start.12 = (f32[8,128]{1,0:T(8,128)S(1)}, f32[8,128]{1,0:T(8,128)S(1)}, u32[]{:S(2)}, u32[]{:S(2)}) collective-permute-start(f32[8,128]{1,0:T(8,128)S(1)} %get-tuple-element.77), channel_id=1, source_target_pairs={{0,1},{1,0},{2,3},{3,2},{4,5},{5,4},{6,7},{7,6},{8,9},{9,8},{10,11... | collective-permute-start | bytes 12296 | tf_op jit(solution)/shard_map/ppermute | solution.py:493
  49.7 3.6 %collective-permute-start.13 = (f32[8,128]{1,0:T(8,128)S(1)}, f32[8,128]{1,0:T(8,128)S(1)}, u32[]{:S(2)}, u32[]{:S(2)}) collective-permute-start(f32[8,128]{1,0:T(8,128)S(1)} %get-tuple-element.78), channel_id=1, source_target_pairs={{0,2},{1,3},{2,0},{3,1},{4,6},{5,7},{6,4},{7,5},{8,10},{9,11},{10,... | collective-permute-start | bytes 12296 | tf_op jit(solution)/shard_map/ppermute | solution.py:493
  50.2 3.2 %collective-permute-start.14 = (f32[8,128]{1,0:T(8,128)S(1)}, f32[8,128]{1,0:T(8,128)S(1)}, u32[]{:S(2)}, u32[]{:S(2)}) collective-permute-start(f32[8,128]{1,0:T(8,128)S(1)} %get-tuple-element.79), channel_id=1, source_target_pairs={{0,3},{1,2},{2,1},{3,0},{4,7},{5,6},{6,5},{7,4},{8,11},{9,10},{10,... | collective-permute-start | bytes 12296 | tf_op jit(solution)/shard_map/ppermute | solution.py:493
  57.1 3.7 %collective-permute-start.15 = (f32[3,512]{1,0:T(4,128)S(1)}, f32[3,512]{1,0:T(4,128)S(1)}, u32[]{:S(2)}, u32[]{:S(2)}) collective-permute-start(f32[3,512]{1,0:T(4,128)S(1)} %get-tuple-element.82), channel_id=1, source_target_pairs={{0,4},{1,5},{2,6},{3,7},{4,0},{5,1},{6,2},{7,3},{8,12},{9,13},{10,... | collective-permute-start | bytes 18440 | tf_op jit(solution)/shard_map/ppermute | solution.py:441
  57.8 3.0 %collective-permute-start.16 = (f32[3,512]{1,0:T(4,128)S(1)}, f32[3,512]{1,0:T(4,128)S(1)}, u32[]{:S(2)}, u32[]{:S(2)}) collective-permute-start(f32[3,512]{1,0:T(4,128)S(1)} %get-tuple-element.83), channel_id=1, source_target_pairs={{0,1},{1,0},{2,3},{3,2},{4,8},{5,9},{6,10},{7,11},{8,4},{9,5},{10,... | collective-permute-start | bytes 18440 | tf_op jit(solution)/shard_map/ppermute | solution.py:441
  57.8 3.0 %collective-permute-start.17 = (f32[3,512]{1,0:T(4,128)S(1)}, f32[3,512]{1,0:T(4,128)S(1)}, u32[]{:S(2)}, u32[]{:S(2)}) collective-permute-start(f32[3,512]{1,0:T(4,128)S(1)} %get-tuple-element.84), channel_id=1, source_target_pairs={{0,1},{1,0},{2,3},{3,2},{4,5},{5,4},{6,7},{7,6},{8,9},{9,8},{10,11... | collective-permute-start | bytes 18440 | tf_op jit(solution)/shard_map/ppermute | solution.py:441
  58.3 3.1 %collective-permute-start.18 = (f32[3,512]{1,0:T(4,128)S(1)}, f32[3,512]{1,0:T(4,128)S(1)}, u32[]{:S(2)}, u32[]{:S(2)}) collective-permute-start(f32[3,512]{1,0:T(4,128)S(1)} %get-tuple-element.85), channel_id=1, source_target_pairs={{0,3},{1,2},{2,1},{3,0},{4,7},{5,6},{6,5},{7,4},{8,11},{9,10},{10,... | collective-permute-start | bytes 18440 | tf_op jit(solution)/shard_map/ppermute | solution.py:441
  65.2 4.0 %collective-permute-start.19 = (f32[3,512]{1,0:T(4,128)S(1)}, f32[3,512]{1,0:T(4,128)S(1)}, u32[]{:S(2)}, u32[]{:S(2)}) collective-permute-start(f32[3,512]{1,0:T(4,128)S(1)} %get-tuple-element.88), channel_id=1, source_target_pairs={{0,4},{1,5},{2,6},{3,7},{4,0},{5,1},{6,2},{7,3},{8,12},{9,13},{10,... | collective-permute-start | bytes 18440 | tf_op jit(solution)/shard_map/ppermute | solution.py:441
  67.6 1.6 %collective-permute-start.20 = (f32[3,512]{1,0:T(4,128)S(1)}, f32[3,512]{1,0:T(4,128)S(1)}, u32[]{:S(2)}, u32[]{:S(2)}) collective-permute-start(f32[3,512]{1,0:T(4,128)S(1)} %get-tuple-element.89), channel_id=1, source_target_pairs={{0,1},{1,0},{2,3},{3,2},{4,8},{5,9},{6,10},{7,11},{8,4},{9,5},{10,... | collective-permute-start | bytes 18440 | tf_op jit(solution)/shard_map/ppermute | solution.py:441
  67.6 1.6 %collective-permute-start.21 = (f32[3,512]{1,0:T(4,128)S(1)}, f32[3,512]{1,0:T(4,128)S(1)}, u32[]{:S(2)}, u32[]{:S(2)}) collective-permute-start(f32[3,512]{1,0:T(4,128)S(1)} %get-tuple-element.90), channel_id=1, source_target_pairs={{0,1},{1,0},{2,3},{3,2},{4,5},{5,4},{6,7},{7,6},{8,9},{9,8},{10,11... | collective-permute-start | bytes 18440 | tf_op jit(solution)/shard_map/ppermute | solution.py:441
  68.1 3.1 %collective-permute-start.22 = (f32[3,512]{1,0:T(4,128)S(1)}, f32[3,512]{1,0:T(4,128)S(1)}, u32[]{:S(2)}, u32[]{:S(2)}) collective-permute-start(f32[3,512]{1,0:T(4,128)S(1)} %get-tuple-element.91), channel_id=1, source_target_pairs={{0,3},{1,2},{2,1},{3,0},{4,7},{5,6},{6,5},{7,4},{8,11},{9,10},{10,... | collective-permute-start | bytes 18440 | tf_op jit(solution)/shard_map/ppermute | solution.py:441
